TPU v7x, 32 devices: a 4x2x2 block of a 4x4x8 slice. The times are simulated.
32 devices in a mesh: dp: 4 (over y, z), pp: 8 (over x, core).
Axes of the slice: x: 4, y: 2, z: 2, core: 2. Of those that a mesh axis runs over, the one named last changes fastest.
The devices are a block of a 4x4x8 slice.
Arguments:
- hidden: bfloat16 [32, 512, 960], P(('dp', 'pp')), parts along dimension 0
- labels: int32 [32, 512], P(('dp', 'pp')), parts along dimension 0
- gamma: float32 [960], replicated
- table: bfloat16 [49152, 960], P('pp')
Outputs:
- output 1: float32 [32, 512], P(('dp', 'pp')), parts along dimension 0
- output 2: bfloat16 [32, 512, 960], P(('dp', 'pp')), parts along dimension 0
- output 3: float32 [4], P('dp'), parts along dimension 0
- output 4: float32 [196608, 960], P(('dp', 'pp')), parts along dimension 0
- output 5: float32 [3840], P('dp'), parts along dimension 0
There are 4 independent parts. A program takes and returns all parts, laid end to end along the dimension named above; an argument that names none is the same for every part.
All inputs are finite; a program needn't handle non-finite values.
Results may differ from a plain program's by a relative error of at most 0.001.
Values are sent between devices in bfloat16 or wider.
A program may use at most 768 MiB of HBM per device.

v0:
```python
import jax
import jax.numpy as jnp
from jax import lax
from jax.sharding import PartitionSpec as P

SOFT_CAP = 30.0
EPS = 1e-6


def norm_rows(rows, gain):
    mean_sq = jnp.mean(rows * rows, axis=-1, keepdims=True)
    return rows * lax.rsqrt(mean_sq + EPS) * (1.0 + gain)


def solution(mesh):
    def local_fn(hidden, labels, gamma, table):
        mb_dev, seq_len, width = hidden.shape
        v_shard = table.shape[0]
        rank = lax.axis_index('pp')
        normed32, norm_vjp = jax.vjp(norm_rows, hidden.astype(jnp.float32), gamma)
        normed = normed32.astype(jnp.bfloat16)
        all_normed = lax.all_gather(normed, 'pp', axis=0, tiled=True)
        all_labels = lax.all_gather(labels, 'pp', axis=0, tiled=True)
        total = all_normed.shape[0] * seq_len
        vocab_ids = rank * v_shard + lax.broadcasted_iota(jnp.int32, (1, v_shard), 1)

        def micro_step(grad_table, scan_in):
            block, block_labels = scan_in
            logits = lax.dot_general(block, table, (((1,), (1,)), ((), ())), preferred_element_type=jnp.float32)
            tanh_z = jnp.tanh(logits / SOFT_CAP)
            capped = SOFT_CAP * tanh_z
            row_max = lax.pmax(jnp.max(capped, axis=1), 'pp')
            label_hit = vocab_ids == block_labels[:, None]
            shifted = jnp.exp(capped - row_max[:, None])
            local_stats = jnp.stack([jnp.sum(shifted, axis=1), jnp.sum(jnp.where(label_hit, capped, 0.0), axis=1)])
            group_stats = lax.psum(local_stats, 'pp')
            tok_loss = row_max + jnp.log(group_stats[0]) - group_stats[1]
            soft_probs = shifted / group_stats[0][:, None]
            grad_capped = jnp.where(label_hit, soft_probs - 1.0, soft_probs) / total
            grad_logits = (grad_capped * (1.0 - tanh_z * tanh_z)).astype(jnp.bfloat16)
            part_dn = jnp.dot(grad_logits, table, preferred_element_type=jnp.float32)
            table_part = lax.dot_general(grad_logits, block, (((0,), (0,)), ((), ())), preferred_element_type=jnp.float32)
            return grad_table + table_part, (tok_loss, part_dn)

        init_acc = jnp.zeros((v_shard, width), jnp.float32)
        grad_table, (all_loss, all_dn) = lax.scan(micro_step, init_acc, (all_normed, all_labels))
        own_dn = lax.psum_scatter(all_dn, 'pp', scatter_dimension=0, tiled=True)
        grad_rows, grad_gain = norm_vjp(own_dn)
        grad_gain = lax.psum(grad_gain, 'pp')
        own_loss = lax.dynamic_slice_in_dim(all_loss, rank * mb_dev, mb_dev, axis=0)
        mean_loss = jnp.reshape(jnp.mean(all_loss), (1,))
        return own_loss, grad_rows.astype(jnp.bfloat16), mean_loss, grad_table, grad_gain

    token_spec = P(('dp', 'pp'))
    return jax.shard_map(local_fn, mesh=mesh,
                         in_specs=(token_spec, token_spec, P(), P('pp')),
                         out_specs=(token_spec, token_spec, P('dp'), token_spec, P('dp')),
                         check_vma=False)
```

profile of v0, /device:TPU:81, one launch (start us, length us, event | category | flops | bytes accessed | tf_op | source)
XLA Modules:
  0.0 871.6 jit_solution(1492748628152851470)
XLA Ops:
  13.2 14.8 %all-gather = s32[8,1,512]{2,1,0:T(1,128)S(1)} all-gather(s32[1,1,512]{2,1,0:T(1,128)} %bitcast.63), channel_id=1, replica_groups=mesh['dp'=4,'pp'=8] {'pp'}, dimensions={0}, use_global_device_ids=true | all-gather | bytes 18432 | tf_op jit(solution)/shard_map/all_gather | solution.py:23
  28.0 34.0 %all-gather.3.cloned.1.call-done = bf16[8,512,960]{1,2,0:T(8,128)(2,1)} async-done(((bf16[1,512,960]{1,2,0:T(8,128)(2,1)}), bf16[8,512,960]{1,2,0:T(8,128)(2,1)}) %all-gather.3.cloned.1.call-update) | async-done | bytes 7864336 | tf_op jit(solution)/shard_map/all_gather | solution.py:22
  62.0 699.7 %while.17 = (s32[]{:T(128)}, f32[6144,960]{0,1:T(8,128)}, f32[8,512]{1,0:T(8,128)S(1)}, f32[8,512,960]{1,2,0:T(8,128)}, s32[8,512]{1,0:T(8,128)S(1)}, /*index=5*...) while((s32[]{:T(128)}, f32[6144,960]{0,1:T(8,128)}, ...), condition=%wide.region_7.8_spmd.clone, body=%wide.region_1.7_spmd.clone.sunk | while | flops 18238152704 | bytes 125208712 | solution.py:46
  62.0 13.5 %fusion.42 = (f32[512]{0:T(512)S(1)}, f32[512,6144]{1,0:T(8,128)}) fusion(bf16[6144,960]{0,1:T(8,128)(2,1)} %get-tuple-element.268, bf16[8,512,960]{1,2,0:T(8,128)(2,1)} %get-tuple-element.267, s32[]{:T(128)S(6)} %copy.21), kind=kOutput, calls=%fused_computation.12.clone.1 | convolution fusion | flops 6049234432 | bytes 25364484 | tf_op jit(solution)/shard_map/while/body/eval_jaxpr/dot_general | solution.py:29
  75.6 12.0 %pmax.12 = f32[512]{0:T(512)S(1)} all-reduce(f32[512]{0:T(512)S(1)} %get-tuple-element.237), channel_id=1, replica_groups=mesh['dp'=4,'pp'=8] {'pp'}, use_global_device_ids=true, to_apply=%region_3.3 | all-reduce | flops 512 | bytes 4096 | tf_op jit(solution)/shard_map/while/body/eval_jaxpr/pmax | solution.py:32
  87.6 8.8 %fusion.43 = (f32[512]{0:T(512)S(1)}, f32[512]{0:T(512)S(1)}) fusion(f32[512,6144]{1,0:T(8,128)} %get-tuple-element.236, f32[512]{0:T(512)S(1)} %pmax.12, s32[512]{0:T(512)S(1)} %bitcast.52, s32[6144]{0:T(1024)S(1)} %bitcast.49), kind=kLoop, calls=%fused_computation.11.clone.1 | loop fusion | flops 22019072 | bytes 12615680 | tf_op jit(solution)/shard_map/while/body/eval_jaxpr/reduce_sum | solution.py:35
  96.4 13.2 %psum.20 = f32[2,512]{1,0:T(2,128)S(1)} all-reduce(f32[2,512]{1,0:T(2,128)S(1)} %pad_maximum_fusion.2), channel_id=1, replica_groups=mesh['dp'=4,'pp'=8] {'pp'}, use_global_device_ids=true, to_apply=%region_6.6 | all-reduce | flops 1024 | bytes 8192 | tf_op jit(solution)/shard_map/while/body/eval_jaxpr/psum | solution.py:36
  109.6 16.4 %bitcast_dynamic-update-slice_fusion.2 = f32[8,512,960]{1,2,0:T(8,128)} fusion(f32[8,512,960]{1,2,0:T(8,128)} %get-tuple-element.255, s32[]{:T(128)S(6)} %copy.21, bf16[6144,960]{0,1:T(8,128)(2,1)} %get-tuple-element.268, f32[512,6144]{1,0:T(8,128)} %get-tuple-element.236, f32[512]{0:T(512)S(1)} %bitcast.59, f32[512]{0:T(512)S(1)} %pmax.12, ...), kind=kOutput, calls=%fused_computation.13.clone.1 | convolution fusion | flops 6077546496 | bytes 26376196 | tf_op jit(solution)/shard_map/while/body/eval_jaxpr/dot_general | solution.py:41
  126.0 17.4 %select_add_fusion.2 = f32[6144,960]{0,1:T(8,128)} fusion(f32[6144,960]{0,1:T(8,128)} %get-tuple-element.253, pred[]{:T(512)S(6)} %compare.3, bf16[8,512,960]{1,2,0:T(8,128)(2,1)} %get-tuple-element.267, s32[]{:T(128)S(6)} %copy.21, f32[512,6144]{1,0:T(8,128)} %get-tuple-element.236, f32[512]{0:T(512)S(1)} %bitcast.60, f32[512]{0:T(512)S(1)} %pmax.12, ...), kind=kOutput, calls=%fused_computation.1.clone.1 | convolution fusion | flops 6089342976 | bytes 60782596 | tf_op jit(solution)/shard_map/while/body/eval_jaxpr/dot_general | solution.py:42
  143.5 13.5 %fusion.42 = (f32[512]{0:T(512)S(1)}, f32[512,6144]{1,0:T(8,128)}) fusion(bf16[6144,960]{0,1:T(8,128)(2,1)} %get-tuple-element.268, bf16[8,512,960]{1,2,0:T(8,128)(2,1)} %get-tuple-element.267, s32[]{:T(128)S(6)} %copy.21), kind=kOutput, calls=%fused_computation.12.clone.1 | convolution fusion | flops 6049234432 | bytes 25364484 | tf_op jit(solution)/shard_map/while/body/eval_jaxpr/dot_general | solution.py:29
  157.0 12.5 %pmax.12 = f32[512]{0:T(512)S(1)} all-reduce(f32[512]{0:T(512)S(1)} %get-tuple-element.237), channel_id=1, replica_groups=mesh['dp'=4,'pp'=8] {'pp'}, use_global_device_ids=true, to_apply=%region_3.3 | all-reduce | flops 512 | bytes 4096 | tf_op jit(solution)/shard_map/while/body/eval_jaxpr/pmax | solution.py:32
  169.5 8.8 %fusion.43 = (f32[512]{0:T(512)S(1)}, f32[512]{0:T(512)S(1)}) fusion(f32[512,6144]{1,0:T(8,128)} %get-tuple-element.236, f32[512]{0:T(512)S(1)} %pmax.12, s32[512]{0:T(512)S(1)} %bitcast.52, s32[6144]{0:T(1024)S(1)} %bitcast.49), kind=kLoop, calls=%fused_computation.11.clone.1 | loop fusion | flops 22019072 | bytes 12615680 | tf_op jit(solution)/shard_map/while/body/eval_jaxpr/reduce_sum | solution.py:35
  178.2 12.5 %psum.20 = f32[2,512]{1,0:T(2,128)S(1)} all-reduce(f32[2,512]{1,0:T(2,128)S(1)} %pad_maximum_fusion.2), channel_id=1, replica_groups=mesh['dp'=4,'pp'=8] {'pp'}, use_global_device_ids=true, to_apply=%region_6.6 | all-reduce | flops 1024 | bytes 8192 | tf_op jit(solution)/shard_map/while/body/eval_jaxpr/psum | solution.py:36
  190.8 16.4 %bitcast_dynamic-update-slice_fusion.2 = f32[8,512,960]{1,2,0:T(8,128)} fusion(f32[8,512,960]{1,2,0:T(8,128)} %get-tuple-element.255, s32[]{:T(128)S(6)} %copy.21, bf16[6144,960]{0,1:T(8,128)(2,1)} %get-tuple-element.268, f32[512,6144]{1,0:T(8,128)} %get-tuple-element.236, f32[512]{0:T(512)S(1)} %bitcast.59, f32[512]{0:T(512)S(1)} %pmax.12, ...), kind=kOutput, calls=%fused_computation.13.clone.1 | convolution fusion | flops 6077546496 | bytes 26376196 | tf_op jit(solution)/shard_map/while/body/eval_jaxpr/dot_general | solution.py:41
  207.3 24.5 %select_add_fusion.2 = f32[6144,960]{0,1:T(8,128)} fusion(f32[6144,960]{0,1:T(8,128)} %get-tuple-element.253, pred[]{:T(512)S(6)} %compare.3, bf16[8,512,960]{1,2,0:T(8,128)(2,1)} %get-tuple-element.267, s32[]{:T(128)S(6)} %copy.21, f32[512,6144]{1,0:T(8,128)} %get-tuple-element.236, f32[512]{0:T(512)S(1)} %bitcast.60, f32[512]{0:T(512)S(1)} %pmax.12, ...), kind=kOutput, calls=%fused_computation.1.clone.1 | convolution fusion | flops 6089342976 | bytes 60782596 | tf_op jit(solution)/shard_map/while/body/eval_jaxpr/dot_general | solution.py:42
  231.8 13.5 %fusion.42 = (f32[512]{0:T(512)S(1)}, f32[512,6144]{1,0:T(8,128)}) fusion(bf16[6144,960]{0,1:T(8,128)(2,1)} %get-tuple-element.268, bf16[8,512,960]{1,2,0:T(8,128)(2,1)} %get-tuple-element.267, s32[]{:T(128)S(6)} %copy.21), kind=kOutput, calls=%fused_computation.12.clone.1 | convolution fusion | flops 6049234432 | bytes 25364484 | tf_op jit(solution)/shard_map/while/body/eval_jaxpr/dot_general | solution.py:29
  245.3 12.5 %pmax.12 = f32[512]{0:T(512)S(1)} all-reduce(f32[512]{0:T(512)S(1)} %get-tuple-element.237), channel_id=1, replica_groups=mesh['dp'=4,'pp'=8] {'pp'}, use_global_device_ids=true, to_apply=%region_3.3 | all-reduce | flops 512 | bytes 4096 | tf_op jit(solution)/shard_map/while/body/eval_jaxpr/pmax | solution.py:32
  257.8 8.8 %fusion.43 = (f32[512]{0:T(512)S(1)}, f32[512]{0:T(512)S(1)}) fusion(f32[512,6144]{1,0:T(8,128)} %get-tuple-element.236, f32[512]{0:T(512)S(1)} %pmax.12, s32[512]{0:T(512)S(1)} %bitcast.52, s32[6144]{0:T(1024)S(1)} %bitcast.49), kind=kLoop, calls=%fused_computation.11.clone.1 | loop fusion | flops 22019072 | bytes 12615680 | tf_op jit(solution)/shard_map/while/body/eval_jaxpr/reduce_sum | solution.py:35
  266.6 12.5 %psum.20 = f32[2,512]{1,0:T(2,128)S(1)} all-reduce(f32[2,512]{1,0:T(2,128)S(1)} %pad_maximum_fusion.2), channel_id=1, replica_groups=mesh['dp'=4,'pp'=8] {'pp'}, use_global_device_ids=true, to_apply=%region_6.6 | all-reduce | flops 1024 | bytes 8192 | tf_op jit(solution)/shard_map/while/body/eval_jaxpr/psum | solution.py:36
  279.2 16.4 %bitcast_dynamic-update-slice_fusion.2 = f32[8,512,960]{1,2,0:T(8,128)} fusion(f32[8,512,960]{1,2,0:T(8,128)} %get-tuple-element.255, s32[]{:T(128)S(6)} %copy.21, bf16[6144,960]{0,1:T(8,128)(2,1)} %get-tuple-element.268, f32[512,6144]{1,0:T(8,128)} %get-tuple-element.236, f32[512]{0:T(512)S(1)} %bitcast.59, f32[512]{0:T(512)S(1)} %pmax.12, ...), kind=kOutput, calls=%fused_computation.13.clone.1 | convolution fusion | flops 6077546496 | bytes 26376196 | tf_op jit(solution)/shard_map/while/body/eval_jaxpr/dot_general | solution.py:41
  295.6 24.5 %select_add_fusion.2 = f32[6144,960]{0,1:T(8,128)} fusion(f32[6144,960]{0,1:T(8,128)} %get-tuple-element.253, pred[]{:T(512)S(6)} %compare.3, bf16[8,512,960]{1,2,0:T(8,128)(2,1)} %get-tuple-element.267, s32[]{:T(128)S(6)} %copy.21, f32[512,6144]{1,0:T(8,128)} %get-tuple-element.236, f32[512]{0:T(512)S(1)} %bitcast.60, f32[512]{0:T(512)S(1)} %pmax.12, ...), kind=kOutput, calls=%fused_computation.1.clone.1 | convolution fusion | flops 6089342976 | bytes 60782596 | tf_op jit(solution)/shard_map/while/body/eval_jaxpr/dot_general | solution.py:42
  320.1 13.5 %fusion.42 = (f32[512]{0:T(512)S(1)}, f32[512,6144]{1,0:T(8,128)}) fusion(bf16[6144,960]{0,1:T(8,128)(2,1)} %get-tuple-element.268, bf16[8,512,960]{1,2,0:T(8,128)(2,1)} %get-tuple-element.267, s32[]{:T(128)S(6)} %copy.21), kind=kOutput, calls=%fused_computation.12.clone.1 | convolution fusion | flops 6049234432 | bytes 25364484 | tf_op jit(solution)/shard_map/while/body/eval_jaxpr/dot_general | solution.py:29
  333.6 12.5 %pmax.12 = f32[512]{0:T(512)S(1)} all-reduce(f32[512]{0:T(512)S(1)} %get-tuple-element.237), channel_id=1, replica_groups=mesh['dp'=4,'pp'=8] {'pp'}, use_global_device_ids=true, to_apply=%region_3.3 | all-reduce | flops 512 | bytes 4096 | tf_op jit(solution)/shard_map/while/body/eval_jaxpr/pmax | solution.py:32
  354.9 12.5 %psum.20 = f32[2,512]{1,0:T(2,128)S(1)} all-reduce(f32[2,512]{1,0:T(2,128)S(1)} %pad_maximum_fusion.2), channel_id=1, replica_groups=mesh['dp'=4,'pp'=8] {'pp'}, use_global_device_ids=true, to_apply=%region_6.6 | all-reduce | flops 1024 | bytes 8192 | tf_op jit(solution)/shard_map/while/body/eval_jaxpr/psum | solution.py:36
  367.5 16.4 %bitcast_dynamic-update-slice_fusion.2 = f32[8,512,960]{1,2,0:T(8,128)} fusion(f32[8,512,960]{1,2,0:T(8,128)} %get-tuple-element.255, s32[]{:T(128)S(6)} %copy.21, bf16[6144,960]{0,1:T(8,128)(2,1)} %get-tuple-element.268, f32[512,6144]{1,0:T(8,128)} %get-tuple-element.236, f32[512]{0:T(512)S(1)} %bitcast.59, f32[512]{0:T(512)S(1)} %pmax.12, ...), kind=kOutput, calls=%fused_computation.13.clone.1 | convolution fusion | flops 6077546496 | bytes 26376196 | tf_op jit(solution)/shard_map/while/body/eval_jaxpr/dot_general | solution.py:41
  383.8 24.5 %select_add_fusion.2 = f32[6144,960]{0,1:T(8,128)} fusion(f32[6144,960]{0,1:T(8,128)} %get-tuple-element.253, pred[]{:T(512)S(6)} %compare.3, bf16[8,512,960]{1,2,0:T(8,128)(2,1)} %get-tuple-element.267, s32[]{:T(128)S(6)} %copy.21, f32[512,6144]{1,0:T(8,128)} %get-tuple-element.236, f32[512]{0:T(512)S(1)} %bitcast.60, f32[512]{0:T(512)S(1)} %pmax.12, ...), kind=kOutput, calls=%fused_computation.1.clone.1 | convolution fusion | flops 6089342976 | bytes 60782596 | tf_op jit(solution)/shard_map/while/body/eval_jaxpr/dot_general | solution.py:42
  408.4 13.5 %fusion.42 = (f32[512]{0:T(512)S(1)}, f32[512,6144]{1,0:T(8,128)}) fusion(bf16[6144,960]{0,1:T(8,128)(2,1)} %get-tuple-element.268, bf16[8,512,960]{1,2,0:T(8,128)(2,1)} %get-tuple-element.267, s32[]{:T(128)S(6)} %copy.21), kind=kOutput, calls=%fused_computation.12.clone.1 | convolution fusion | flops 6049234432 | bytes 25364484 | tf_op jit(solution)/shard_map/while/body/eval_jaxpr/dot_general | solution.py:29
  421.9 12.5 %pmax.12 = f32[512]{0:T(512)S(1)} all-reduce(f32[512]{0:T(512)S(1)} %get-tuple-element.237), channel_id=1, replica_groups=mesh['dp'=4,'pp'=8] {'pp'}, use_global_device_ids=true, to_apply=%region_3.3 | all-reduce | flops 512 | bytes 4096 | tf_op jit(solution)/shard_map/while/body/eval_jaxpr/pmax | solution.py:32
  443.2 12.5 %psum.20 = f32[2,512]{1,0:T(2,128)S(1)} all-reduce(f32[2,512]{1,0:T(2,128)S(1)} %pad_maximum_fusion.2), channel_id=1, replica_groups=mesh['dp'=4,'pp'=8] {'pp'}, use_global_device_ids=true, to_apply=%region_6.6 | all-reduce | flops 1024 | bytes 8192 | tf_op jit(solution)/shard_map/while/body/eval_jaxpr/psum | solution.py:36
  455.8 16.4 %bitcast_dynamic-update-slice_fusion.2 = f32[8,512,960]{1,2,0:T(8,128)} fusion(f32[8,512,960]{1,2,0:T(8,128)} %get-tuple-element.255, s32[]{:T(128)S(6)} %copy.21, bf16[6144,960]{0,1:T(8,128)(2,1)} %get-tuple-element.268, f32[512,6144]{1,0:T(8,128)} %get-tuple-element.236, f32[512]{0:T(512)S(1)} %bitcast.59, f32[512]{0:T(512)S(1)} %pmax.12, ...), kind=kOutput, calls=%fused_computation.13.clone.1 | convolution fusion | flops 6077546496 | bytes 26376196 | tf_op jit(solution)/shard_map/while/body/eval_jaxpr/dot_general | solution.py:41
  472.2 24.5 %select_add_fusion.2 = f32[6144,960]{0,1:T(8,128)} fusion(f32[6144,960]{0,1:T(8,128)} %get-tuple-element.253, pred[]{:T(512)S(6)} %compare.3, bf16[8,512,960]{1,2,0:T(8,128)(2,1)} %get-tuple-element.267, s32[]{:T(128)S(6)} %copy.21, f32[512,6144]{1,0:T(8,128)} %get-tuple-element.236, f32[512]{0:T(512)S(1)} %bitcast.60, f32[512]{0:T(512)S(1)} %pmax.12, ...), kind=kOutput, calls=%fused_computation.1.clone.1 | convolution fusion | flops 6089342976 | bytes 60782596 | tf_op jit(solution)/shard_map/while/body/eval_jaxpr/dot_general | solution.py:42
  496.7 13.5 %fusion.42 = (f32[512]{0:T(512)S(1)}, f32[512,6144]{1,0:T(8,128)}) fusion(bf16[6144,960]{0,1:T(8,128)(2,1)} %get-tuple-element.268, bf16[8,512,960]{1,2,0:T(8,128)(2,1)} %get-tuple-element.267, s32[]{:T(128)S(6)} %copy.21), kind=kOutput, calls=%fused_computation.12.clone.1 | convolution fusion | flops 6049234432 | bytes 25364484 | tf_op jit(solution)/shard_map/while/body/eval_jaxpr/dot_general | solution.py:29
  510.2 12.5 %pmax.12 = f32[512]{0:T(512)S(1)} all-reduce(f32[512]{0:T(512)S(1)} %get-tuple-element.237), channel_id=1, replica_groups=mesh['dp'=4,'pp'=8] {'pp'}, use_global_device_ids=true, to_apply=%region_3.3 | all-reduce | flops 512 | bytes 4096 | tf_op jit(solution)/shard_map/while/body/eval_jaxpr/pmax | solution.py:32
  531.5 12.5 %psum.20 = f32[2,512]{1,0:T(2,128)S(1)} all-reduce(f32[2,512]{1,0:T(2,128)S(1)} %pad_maximum_fusion.2), channel_id=1, replica_groups=mesh['dp'=4,'pp'=8] {'pp'}, use_global_device_ids=true, to_apply=%region_6.6 | all-reduce | flops 1024 | bytes 8192 | tf_op jit(solution)/shard_map/while/body/eval_jaxpr/psum | solution.py:36
  544.1 16.4 %bitcast_dynamic-update-slice_fusion.2 = f32[8,512,960]{1,2,0:T(8,128)} fusion(f32[8,512,960]{1,2,0:T(8,128)} %get-tuple-element.255, s32[]{:T(128)S(6)} %copy.21, bf16[6144,960]{0,1:T(8,128)(2,1)} %get-tuple-element.268, f32[512,6144]{1,0:T(8,128)} %get-tuple-element.236, f32[512]{0:T(512)S(1)} %bitcast.59, f32[512]{0:T(512)S(1)} %pmax.12, ...), kind=kOutput, calls=%fused_computation.13.clone.1 | convolution fusion | flops 6077546496 | bytes 26376196 | tf_op jit(solution)/shard_map/while/body/eval_jaxpr/dot_general | solution.py:41
  560.5 24.6 %select_add_fusion.2 = f32[6144,960]{0,1:T(8,128)} fusion(f32[6144,960]{0,1:T(8,128)} %get-tuple-element.253, pred[]{:T(512)S(6)} %compare.3, bf16[8,512,960]{1,2,0:T(8,128)(2,1)} %get-tuple-element.267, s32[]{:T(128)S(6)} %copy.21, f32[512,6144]{1,0:T(8,128)} %get-tuple-element.236, f32[512]{0:T(512)S(1)} %bitcast.60, f32[512]{0:T(512)S(1)} %pmax.12, ...), kind=kOutput, calls=%fused_computation.1.clone.1 | convolution fusion | flops 6089342976 | bytes 60782596 | tf_op jit(solution)/shard_map/while/body/eval_jaxpr/dot_general | solution.py:42
  585.1 13.5 %fusion.42 = (f32[512]{0:T(512)S(1)}, f32[512,6144]{1,0:T(8,128)}) fusion(bf16[6144,960]{0,1:T(8,128)(2,1)} %get-tuple-element.268, bf16[8,512,960]{1,2,0:T(8,128)(2,1)} %get-tuple-element.267, s32[]{:T(128)S(6)} %copy.21), kind=kOutput, calls=%fused_computation.12.clone.1 | convolution fusion | flops 6049234432 | bytes 25364484 | tf_op jit(solution)/shard_map/while/body/eval_jaxpr/dot_general | solution.py:29
  598.6 12.5 %pmax.12 = f32[512]{0:T(512)S(1)} all-reduce(f32[512]{0:T(512)S(1)} %get-tuple-element.237), channel_id=1, replica_groups=mesh['dp'=4,'pp'=8] {'pp'}, use_global_device_ids=true, to_apply=%region_3.3 | all-reduce | flops 512 | bytes 4096 | tf_op jit(solution)/shard_map/while/body/eval_jaxpr/pmax | solution.py:32
  619.9 12.5 %psum.20 = f32[2,512]{1,0:T(2,128)S(1)} all-reduce(f32[2,512]{1,0:T(2,128)S(1)} %pad_maximum_fusion.2), channel_id=1, replica_groups=mesh['dp'=4,'pp'=8] {'pp'}, use_global_device_ids=true, to_apply=%region_6.6 | all-reduce | flops 1024 | bytes 8192 | tf_op jit(solution)/shard_map/while/body/eval_jaxpr/psum | solution.py:36
  632.5 16.4 %bitcast_dynamic-update-slice_fusion.2 = f32[8,512,960]{1,2,0:T(8,128)} fusion(f32[8,512,960]{1,2,0:T(8,128)} %get-tuple-element.255, s32[]{:T(128)S(6)} %copy.21, bf16[6144,960]{0,1:T(8,128)(2,1)} %get-tuple-element.268, f32[512,6144]{1,0:T(8,128)} %get-tuple-element.236, f32[512]{0:T(512)S(1)} %bitcast.59, f32[512]{0:T(512)S(1)} %pmax.12, ...), kind=kOutput, calls=%fused_computation.13.clone.1 | convolution fusion | flops 6077546496 | bytes 26376196 | tf_op jit(solution)/shard_map/while/body/eval_jaxpr/dot_general | solution.py:41
  648.9 24.5 %select_add_fusion.2 = f32[6144,960]{0,1:T(8,128)} fusion(f32[6144,960]{0,1:T(8,128)} %get-tuple-element.253, pred[]{:T(512)S(6)} %compare.3, bf16[8,512,960]{1,2,0:T(8,128)(2,1)} %get-tuple-element.267, s32[]{:T(128)S(6)} %copy.21, f32[512,6144]{1,0:T(8,128)} %get-tuple-element.236, f32[512]{0:T(512)S(1)} %bitcast.60, f32[512]{0:T(512)S(1)} %pmax.12, ...), kind=kOutput, calls=%fused_computation.1.clone.1 | convolution fusion | flops 6089342976 | bytes 60782596 | tf_op jit(solution)/shard_map/while/body/eval_jaxpr/dot_general | solution.py:42
  673.4 13.5 %fusion.42 = (f32[512]{0:T(512)S(1)}, f32[512,6144]{1,0:T(8,128)}) fusion(bf16[6144,960]{0,1:T(8,128)(2,1)} %get-tuple-element.268, bf16[8,512,960]{1,2,0:T(8,128)(2,1)} %get-tuple-element.267, s32[]{:T(128)S(6)} %copy.21), kind=kOutput, calls=%fused_computation.12.clone.1 | convolution fusion | flops 6049234432 | bytes 25364484 | tf_op jit(solution)/shard_map/while/body/eval_jaxpr/dot_general | solution.py:29
  686.9 12.5 %pmax.12 = f32[512]{0:T(512)S(1)} all-reduce(f32[512]{0:T(512)S(1)} %get-tuple-element.237), channel_id=1, replica_groups=mesh['dp'=4,'pp'=8] {'pp'}, use_global_device_ids=true, to_apply=%region_3.3 | all-reduce | flops 512 | bytes 4096 | tf_op jit(solution)/shard_map/while/body/eval_jaxpr/pmax | solution.py:32
  708.2 12.5 %psum.20 = f32[2,512]{1,0:T(2,128)S(1)} all-reduce(f32[2,512]{1,0:T(2,128)S(1)} %pad_maximum_fusion.2), channel_id=1, replica_groups=mesh['dp'=4,'pp'=8] {'pp'}, use_global_device_ids=true, to_apply=%region_6.6 | all-reduce | flops 1024 | bytes 8192 | tf_op jit(solution)/shard_map/while/body/eval_jaxpr/psum | solution.py:36
  720.8 16.4 %bitcast_dynamic-update-slice_fusion.2 = f32[8,512,960]{1,2,0:T(8,128)} fusion(f32[8,512,960]{1,2,0:T(8,128)} %get-tuple-element.255, s32[]{:T(128)S(6)} %copy.21, bf16[6144,960]{0,1:T(8,128)(2,1)} %get-tuple-element.268, f32[512,6144]{1,0:T(8,128)} %get-tuple-element.236, f32[512]{0:T(512)S(1)} %bitcast.59, f32[512]{0:T(512)S(1)} %pmax.12, ...), kind=kOutput, calls=%fused_computation.13.clone.1 | convolution fusion | flops 6077546496 | bytes 26376196 | tf_op jit(solution)/shard_map/while/body/eval_jaxpr/dot_general | solution.py:41
  737.2 24.5 %select_add_fusion.2 = f32[6144,960]{0,1:T(8,128)} fusion(f32[6144,960]{0,1:T(8,128)} %get-tuple-element.253, pred[]{:T(512)S(6)} %compare.3, bf16[8,512,960]{1,2,0:T(8,128)(2,1)} %get-tuple-element.267, s32[]{:T(128)S(6)} %copy.21, f32[512,6144]{1,0:T(8,128)} %get-tuple-element.236, f32[512]{0:T(512)S(1)} %bitcast.60, f32[512]{0:T(512)S(1)} %pmax.12, ...), kind=kOutput, calls=%fused_computation.1.clone.1 | convolution fusion | flops 6089342976 | bytes 60782596 | tf_op jit(solution)/shard_map/while/body/eval_jaxpr/dot_general | solution.py:42
  763.6 81.2 %reduce-scatter.2.cloned.1.call-done = f32[1,512,960]{1,2,0:T(8,128)} async-done(((f32[8,512,960]{1,2,0:T(8,128)}), f32[1,512,960]{1,2,0:T(8,128)}) %reduce-scatter.2.cloned.1.call-update) | async-done | bytes 1966096 | tf_op jit(solution)/shard_map/reduce_scatter | solution.py:47
  847.1 13.5 %psum.17 = f32[960]{0:T(1024)} all-reduce(f32[960]{0:T(1024)S(1)} %get-tuple-element.159), channel_id=1, replica_groups=mesh['dp'=4,'pp'=8] {'pp'}, use_global_device_ids=true, to_apply=%region_12.13 | all-reduce | flops 960 | bytes 7680 | tf_op jit(solution)/shard_map/psum | solution.py:49
  (84 shorter events, 57.2 us)
Async XLA Ops:
  7.2 54.8 %all-gather.3.cloned.1.call-start = ((), (), s32[]{:S(2)}) async-start(), calls=%async_computation.1 | async-start | bytes 8847360 | tf_op jit(solution)/shard_map/all_gather | solution.py:22
  8.7 0.6 copy-start.5
  9.3 0.7 copy-start.3
  10.0 0.6 copy-start.1
  13.1 831.7 %reduce-scatter.2.cloned.1.call-start = ((), (), s32[]{:S(2)}) async-start(), calls=%async_computation.2 | async-start | bytes 17694720 | tf_op jit(solution)/shard_map/reduce_scatter | solution.py:47
  761.7 83.1 %copy-start = (bf16[1,512,960]{1,2,0:T(8,128)(2,1)S(1)}, bf16[1,512,960]{1,2,0:T(8,128)(2,1)}, u32[]{:S(2)}) copy-start(bf16[1,512,960]{1,2,0:T(8,128)(2,1)} %param.6) | copy-start | bytes 2949124
  761.7 83.1 %copy-start.2 = (f32[960]{0:T(1024)S(1)}, f32[960]{0:T(1024)}, u32[]{:S(2)}) copy-start(f32[960]{0:T(1024)} %copy-done.1) | copy-start | bytes 11524
  761.7 83.1 %copy-start.4 = (f32[512]{0:T(512)S(1)}, f32[512]{0:T(512)}, u32[]{:S(2)}) copy-start(f32[512]{0:T(512)} %copy-done.3) | copy-start | bytes 6148
  761.7 99.0 %copy-start.6 = (f32[512]{0:T(512)S(1)}, f32[512]{0:T(512)}, u32[]{:S(2)}) copy-start(f32[512]{0:T(512)} %copy-done.5) | copy-start | bytes 6148
Sparse Core Ops, SparseCore 0:
  13.2 48.7 all-gather.2
  761.9 82.8 reduce-scatter.1
where the time goes:
time: 872 us
  matrix products  428 us (49%)
  blocking collectives  228 us (26%)
  waiting for transfers between devices  115 us (13%)
  other arithmetic  80.9 us (9%)
  between operations  15.9 us (2%)
    dot_general x8, matrix products, micro_step(): lax.dot_general(grad_logits, block, (((0,), (0,)), ((), ())), preferred_e...  189 us
    dot_general x8, matrix products, micro_step(): part_dn = jnp.dot(grad_logits, table, preferred_element_type=jnp.float32)  131 us
    dot_general x8, matrix products, micro_step(): lax.dot_general(block, table, (((1,), (1,)), ((), ())), preferred_element...  108 us
    psum x8, blocking collectives, micro_step(): group_stats = lax.psum(local_stats, 'pp')  101 us
    pmax x8, blocking collectives, micro_step(): row_max = lax.pmax(jnp.max(capped, axis=1), 'pp')  99.3 us
    reduce_scatter x1, waiting for transfers between devices, local_fn(): own_dn = lax.psum_scatter(all_dn, 'pp', scatter_dimension=0, tiled=True)  81.2 us
    reduce_sum x8, other arithmetic, micro_step(): jnp.sum(shifted, axis=1)  70.2 us
    all_gather x1, waiting for transfers between devices, local_fn(): all_normed = lax.all_gather(normed, 'pp', axis=0, tiled=True)  34 us
  transfers between devices with their start and end apart: 2, of which 2 were waited for; matrix products, arithmetic and copies ran while one was open for 0% of the time, Pallas kernels for 0%

commit v1 on v0

v1 whole, which is shorter than its diff:
```python
import functools
import math

import jax
import jax.numpy as jnp
from jax import lax
from jax.experimental import pallas as pl
from jax.experimental.pallas import tpu as pltpu
from jax.sharding import PartitionSpec as P

SOFT_CAP = 30.0
EPS = 1e-6
CAP_LOG2E = SOFT_CAP * math.log2(math.e)
FWD_TILE = 1536
FWD_SUB = 512
BWD_TILE = 1024
BWD_SUB = 512
VMEM_LIMIT = 66_000_000


def norm_rows(rows, gain):
    mean_sq = jnp.mean(rows * rows, axis=-1, keepdims=True)
    return rows * lax.rsqrt(mean_sq + EPS) * (1.0 + gain)


def fold8(x):
    return jnp.sum(x.reshape(x.shape[0] // 8, 8, x.shape[1]), axis=0)


def fwd_kernel(n_tiles, labels_ref, normed_ref, w_hbm, t_ref, stats_ref, w_ref, w_sems):
    chunk, tile = pl.program_id(0), pl.program_id(1)

    def w_copy(i):
        rows = pl.ds(i * FWD_TILE, FWD_TILE)
        return pltpu.make_async_copy(w_hbm.at[rows, :], w_ref.at[rows, :], w_sems.at[i])

    @pl.when(chunk == 0)
    def _():
        @pl.when(tile == 0)
        def _():
            for i in range(n_tiles):
                w_copy(i).start()
        w_copy(tile).wait()

    @pl.when(tile == 0)
    def _():
        stats_ref[...] = jnp.zeros_like(stats_ref)

    row0 = pl.multiple_of(tile * FWD_TILE, FWD_TILE)
    normed = normed_ref[...]
    labels = labels_ref[...] - row0
    iota = lax.broadcasted_iota(jnp.int32, (FWD_SUB, normed.shape[0]), 0)
    exp_sum = stats_ref[0:8, :]
    label_sum = stats_ref[8:16, :]
    for s in range(FWD_TILE // FWD_SUB):
        w = w_ref[pl.ds(pl.multiple_of(row0 + s * FWD_SUB, FWD_SUB), FWD_SUB), :]
        z = lax.dot_general(w, normed, (((1,), (1,)), ((), ())), preferred_element_type=jnp.float32)
        t = jnp.tanh(z * (1.0 / SOFT_CAP))
        t_ref[s * FWD_SUB:(s + 1) * FWD_SUB, :] = t
        exp_sum += fold8(jnp.exp2(t * CAP_LOG2E))
        label_sum += fold8(jnp.where(iota == labels - s * FWD_SUB, t, 0.0))
    stats_ref[0:8, :] = exp_sum
    stats_ref[8:16, :] = label_sum


def forward(normed, labels, table):
    tokens, width = normed.shape
    vocab = table.shape[0]
    chunk = 512
    n_tiles = vocab // FWD_TILE
    return pl.pallas_call(
        functools.partial(fwd_kernel, n_tiles),
        grid=(tokens // chunk, n_tiles),
        in_specs=[
            pl.BlockSpec((1, chunk), lambda c, v: (0, c)),
            pl.BlockSpec((chunk, width), lambda c, v: (c, 0)),
            pl.BlockSpec(memory_space=pl.ANY),
        ],
        out_specs=[
            pl.BlockSpec((FWD_TILE, chunk), lambda c, v: (v, c)),
            pl.BlockSpec((16, chunk), lambda c, v: (0, c)),
        ],
        out_shape=[
            jax.ShapeDtypeStruct((vocab, tokens), jnp.float32),
            jax.ShapeDtypeStruct((16, tokens), jnp.float32),
        ],
        scratch_shapes=[pltpu.VMEM((vocab, width), table.dtype), pltpu.SemaphoreType.DMA((n_tiles,))],
        compiler_params=pltpu.CompilerParams(vmem_limit_bytes=VMEM_LIMIT),
        cost_estimate=pl.CostEstimate(flops=2 * tokens * vocab * width, transcendentals=2 * tokens * vocab,
                                      bytes_accessed=4 * tokens * vocab),
        name='head_fwd',
    )(labels, normed, table)


def bwd_kernel(n_chunks, n_tiles, total, labels_ref, inv_ref, normed_ref, t_ref, wt_ref, dn_ref, dw_hbm, dw_ref, dw_sems):
    chunk, tile = pl.program_id(0), pl.program_id(1)
    row0 = pl.multiple_of(tile * BWD_TILE, BWD_TILE)
    tile_rows = pl.ds(row0, BWD_TILE)

    @pl.when(tile == 0)
    def _():
        dn_ref[...] = jnp.zeros_like(dn_ref)

    @pl.when(chunk == 0)
    def _():
        dw_ref[tile_rows, :] = jnp.zeros((BWD_TILE, dw_ref.shape[1]), jnp.float32)

    normed = normed_ref[...]
    labels = labels_ref[...] - row0
    inv = inv_ref[...]
    iota = lax.broadcasted_iota(jnp.int32, (BWD_SUB, normed.shape[0]), 0)
    dz = []
    for s in range(BWD_TILE // BWD_SUB):
        t = t_ref[s * BWD_SUB:(s + 1) * BWD_SUB, :]
        p = jnp.exp2(t * CAP_LOG2E) * inv
        dc = jnp.where(iota == labels - s * BWD_SUB, p - 1.0 / total, p)
        dz.append((dc * (1.0 - t * t)).astype(jnp.bfloat16))
        rows = pl.ds(pl.multiple_of(row0 + s * BWD_SUB, BWD_SUB), BWD_SUB)
        dw_ref[rows, :] += jnp.dot(dz[-1], normed, preferred_element_type=jnp.float32)
    dz = jnp.concatenate(dz, axis=0)
    dn_ref[...] += jnp.dot(wt_ref[...], dz, preferred_element_type=jnp.float32)

    @pl.when(chunk == n_chunks - 1)
    def _():
        pltpu.make_async_copy(dw_ref.at[tile_rows, :], dw_hbm.at[tile_rows, :], dw_sems.at[tile]).start()

        @pl.when(tile == n_tiles - 1)
        def _():
            for i in range(n_tiles):
                rows = pl.ds(i * BWD_TILE, BWD_TILE)
                pltpu.make_async_copy(dw_ref.at[rows, :], dw_hbm.at[rows, :], dw_sems.at[i]).wait()


def backward(t, normed, labels, inv, table_t):
    vocab, tokens = t.shape
    width = normed.shape[1]
    chunk = 512
    n_chunks, n_tiles = tokens // chunk, vocab // BWD_TILE
    return pl.pallas_call(
        functools.partial(bwd_kernel, n_chunks, n_tiles, tokens),
        grid=(n_chunks, n_tiles),
        in_specs=[
            pl.BlockSpec((1, chunk), lambda c, v: (0, c)),
            pl.BlockSpec((1, chunk), lambda c, v: (0, c)),
            pl.BlockSpec((chunk, width), lambda c, v: (c, 0)),
            pl.BlockSpec((BWD_TILE, chunk), lambda c, v: (v, c)),
            pl.BlockSpec((width, BWD_TILE), lambda c, v: (0, v)),
        ],
        out_specs=[
            pl.BlockSpec((None, width, chunk), lambda c, v: (c, 0, 0)),
            pl.BlockSpec(memory_space=pl.ANY),
        ],
        out_shape=[
            jax.ShapeDtypeStruct((n_chunks, width, chunk), jnp.float32),
            jax.ShapeDtypeStruct((vocab, width), jnp.float32),
        ],
        scratch_shapes=[pltpu.VMEM((vocab, width), jnp.float32), pltpu.SemaphoreType.DMA((n_tiles,))],
        compiler_params=pltpu.CompilerParams(vmem_limit_bytes=VMEM_LIMIT),
        cost_estimate=pl.CostEstimate(flops=4 * tokens * vocab * width, transcendentals=tokens * vocab,
                                      bytes_accessed=4 * tokens * vocab),
        name='head_bwd',
    )(labels, inv, normed, t, table_t)


def solution(mesh):
    def local_fn(hidden, labels, gamma, table):
        mb_dev, seq_len, width = hidden.shape
        v_shard = table.shape[0]
        rank = lax.axis_index('pp')
        own = mb_dev * seq_len
        normed32, norm_vjp = jax.vjp(norm_rows, hidden.astype(jnp.float32).reshape(own, width), gamma)
        normed = lax.all_gather(normed32.astype(jnp.bfloat16), 'pp', axis=0, tiled=True)
        all_labels = lax.all_gather(labels.reshape(1, own), 'pp', axis=1, tiled=True)
        total = normed.shape[0]
        local_labels = all_labels - rank * v_shard
        t, stats = forward(normed, local_labels, table)
        stats = lax.psum(jnp.sum(stats.reshape(2, 8, total), axis=1), 'pp')
        all_loss = jnp.log(stats[0]) - SOFT_CAP * stats[1]
        inv = (1.0 / (stats[0] * total))[None, :]
        dn, grad_table = backward(t, normed, local_labels, inv, table.T)
        own_dn = lax.psum_scatter(dn, 'pp', scatter_dimension=0, tiled=True)[0].T
        grad_rows, grad_gain = norm_vjp(own_dn)
        grad_gain = lax.psum(grad_gain, 'pp')
        own_loss = lax.dynamic_slice_in_dim(all_loss, rank * own, own, axis=0).reshape(mb_dev, seq_len)
        mean_loss = jnp.reshape(jnp.mean(all_loss), (1,))
        grad_hidden = grad_rows.astype(jnp.bfloat16).reshape(mb_dev, seq_len, width)
        return own_loss, grad_hidden, mean_loss, grad_table, grad_gain

    token_spec = P(('dp', 'pp'))
    return jax.shard_map(local_fn, mesh=mesh,
                         in_specs=(token_spec, token_spec, P(), P('pp')),
                         out_specs=(token_spec, token_spec, P('dp'), token_spec, P('dp')),
                         check_vma=False)
```

time: 872 us -> 437 us (0.50)
  matrix products: 428 us -> 0 us
  Pallas kernels: 0 us -> 216 us
  blocking collectives: 228 us -> 49.2 us
  other arithmetic: 80.9 us -> 8.2 us
  local copies, waits for them, and re-layouts: 2.39 us -> 62.2 us
  waiting for transfers between devices: 115 us -> 84.6 us
    dot_general x24 -> x0, matrix products: 428 us -> none  [the longest x8 189 us: micro_step(): lax.dot_general(grad_logits, block, (((0,), (0,)), ((), ())), preferred_e...]
    pallas_call x0 -> x2, Pallas kernels: none -> 216 us  [the longest x1 134 us: backward(): pl.pallas_call(functools.partial(bwd_kernel, n_chunks, n_tiles, tokens),...]
    pmax x8 -> x0, blocking collectives: 99.3 us -> none  [micro_step(): row_max = lax.pmax(jnp.max(capped, axis=1), 'pp')]
    psum x8 -> x1, blocking collectives: 101 us -> 20.9 us  [local_fn(): stats = lax.psum(jnp.sum(stats.reshape(2, 8, total), axis=1), 'pp')]
    reduce_sum x8 -> x1, other arithmetic: 70.2 us -> 1.04 us  [local_fn(): stats = lax.psum(jnp.sum(stats.reshape(2, 8, total), axis=1), 'pp')]
    unnamed x15 -> x24, local copies, waits for them, and re-layouts: 1.2 us -> 44.4 us
    pallas_call x0 -> x1, local copies, waits for them, and re-layouts: none -> 17.2 us  [backward(): pl.pallas_call(functools.partial(bwd_kernel, n_chunks, n_tiles, tokens),...]
    reduce_scatter x1, waiting for transfers between devices: 81.2 us -> 65 us  [local_fn(): own_dn = lax.psum_scatter(dn, 'pp', scatter_dimension=0, tiled=True)[0].T]
  transfers between devices with their start and end apart: 2 -> 2, of which waited for: 2 -> 2; matrix products, arithmetic and copies ran while one was open for 0% -> 10% of each run, Pallas kernels for 0% -> 0%
where the time goes in v1:
time: 437 us; the launch traced here: 436 us
  Pallas kernels  216 us (49%)
  waiting for transfers between devices  84.6 us (19%)
  local copies, waits for them, and re-layouts  62.2 us (14%)
  blocking collectives  49.2 us (11%)
  between operations  16 us (4%)
  other arithmetic  8.2 us (2%)
    pallas_call x1, Pallas kernels, backward(): pl.pallas_call(functools.partial(bwd_kernel, n_chunks, n_tiles, tokens),...  134 us
    pallas_call x1, Pallas kernels, forward(): pl.pallas_call(functools.partial(fwd_kernel, n_tiles), grid=(tokens // ch...  81.6 us
    reduce_scatter x1, waiting for transfers between devices, local_fn(): own_dn = lax.psum_scatter(dn, 'pp', scatter_dimension=0, tiled=True)[0].T  65 us
    unnamed x24, local copies, waits for them, and re-layouts  44.4 us
    psum x1, blocking collectives, local_fn(): stats = lax.psum(jnp.sum(stats.reshape(2, 8, total), axis=1), 'pp')  20.9 us
    all_gather x1, waiting for transfers between devices, local_fn(): lax.all_gather(normed32.astype(jnp.bfloat16), 'pp', axis=0, tiled=True)  19.6 us
    pallas_call x1, local copies, waits for them, and re-layouts, backward(): pl.pallas_call(functools.partial(bwd_kernel, n_chunks, n_tiles, tokens),...  17.2 us
    all_gather x1, blocking collectives, local_fn(): lax.all_gather(labels.reshape(1, own), 'pp', axis=1, tiled=True)  14.8 us
  transfers between devices with their start and end apart: 2, of which 2 were waited for; matrix products, arithmetic and copies ran while one was open for 10% of the time, Pallas kernels for 0%

profile of v1, /device:TPU:81, one launch (start us, length us, event | category | flops | bytes accessed | tf_op | source)
XLA Modules:
  0.0 436.2 jit_solution(1026640702631499041)
XLA Ops:
  7.2 0.1 all-gather.2.cloned.1.call-start
  7.2 1.5 copy.9
  8.7 0.0 copy-start
  8.7 0.7 broadcast_add_fusion
  9.5 0.0 copy-start.3
  9.5 0.3 fusion.5
  9.7 0.0 copy-start.7
  9.8 0.6 copy-done.7
  10.3 0.0 copy-done.3
  10.3 0.0 copy-start.5
  10.4 0.6 copy-done.5
  10.9 1.3 fusion.2
  12.2 0.1 all-gather.2.cloned.1.call-update
  12.3 0.0 copy-done
  12.3 0.1 reduce-scatter.2.cloned.1.call-start
  12.4 0.0 copy-start.9
  12.4 16.4 %copy.10.w_hbm = bf16[6144,960]{1,0:T(8,128)(2,1)} copy(bf16[6144,960]{0,1:T(8,128)(2,1)} %param.7) | data formatting | bytes 23592960 | tf_op args[3]
  28.7 0.0 copy-done.9
  28.7 14.8 %all_gather.6 = s32[1,4096]{1,0:T(1,128)S(1)} all-gather(s32[1,512]{1,0:T(1,128)S(1)} %copy-done.9), channel_id=1, replica_groups=mesh['dp'=4,'pp'=8] {'pp'}, dimensions={1}, use_global_device_ids=true | all-gather | bytes 18432 | tf_op jit(solution)/shard_map/all_gather | solution.py:173
  43.6 0.6 broadcast_subtract_fusion.labels_ref
  44.2 19.6 %all-gather.2.cloned.1.call-done.normed_ref = bf16[4096,960]{1,0:T(8,128)(2,1)} async-done(((bf16[512,960]{1,0:T(8,128)(2,1)}), bf16[4096,960]{1,0:T(8,128)(2,1)}) %all-gather.2.cloned.1.call-update) | async-done | bytes 7864336 | tf_op jit(solution)/shard_map/all_gather | solution.py:172
  63.7 81.6 %head_fwd.1 = (f32[6144,4096]{1,0:T(8,128)}, f32[16,4096]{1,0:T(8,128)}) custom-call(s32[1,4096]{1,0:T(1,128)} %broadcast_subtract_fusion.labels_ref, bf16[4096,960]{1,0:T(8,128)(2,1)} %all-gather.2.cloned.1.call-done.normed_ref, bf16[6144,960]{1,0:T(8,128)(2,1)} %copy.10.w_hbm), custom_call_target="tpu_custom_call" | custom-call | flops 48318382080 | bytes 100663296 | tf_op jit(solution)/shard_map/head_fwd/pallas_call | solution.py:71
  145.3 1.0 bitcast_reduce_fusion
  146.3 20.9 %psum.14 = f32[2,4096]{1,0:T(2,128)S(1)} all-reduce(f32[2,4096]{1,0:T(2,128)S(1)} %bitcast_reduce_fusion), channel_id=1, replica_groups=mesh['dp'=4,'pp'=8] {'pp'}, use_global_device_ids=true, to_apply=%region_2.0 | all-reduce | flops 8192 | bytes 65536 | tf_op jit(solution)/shard_map/psum | solution.py:177
  167.2 1.2 fusion.10
  168.5 134.3 %head_bwd.1 = (f32[8,960,512]{2,1,0:T(8,128)}, f32[6144,960]{1,0:T(8,128)}) custom-call(s32[1,4096]{1,0:T(1,128)} %broadcast_subtract_fusion.labels_ref, f32[1,4096]{1,0:T(1,128)} %get-tuple-element.22.inv_ref, bf16[4096,960]{1,0:T(8,128)(2,1)} %all-gather.2.cloned.1.call-done.normed_ref, f32[6144,4096]{1,0:T(8,128)} %get-tuple-element.10.t_ref, ...), custom_call_target="tpu_custom_call" | custom-call | flops 96636764160 | bytes 100663296 | tf_op jit(solution)/shard_map/head_bwd/pallas_call | solution.py:139
  302.8 17.2 %copy.11 = f32[8,960,512]{1,2,0:T(8,128)} copy(f32[8,960,512]{2,1,0:T(8,128)} %get-tuple-element.11) | data formatting | bytes 31457280 | tf_op jit(solution)/shard_map/head_bwd/pallas_call | solution.py:139
  320.0 0.1 reduce-scatter.2.cloned.1.call-update
  320.0 0.0 copy-start.1
  320.1 0.0 copy-start.4
  320.1 0.0 copy-start.6
  320.1 24.1 %copy.13 = f32[6144,960]{0,1:T(8,128)} copy(f32[6144,960]{1,0:T(8,128)} %get-tuple-element.16) | data formatting | bytes 47185920
  344.2 0.0 copy-start.8
  344.8 0.6 constant_dynamic-slice_fusion
  345.4 65.0 %reduce-scatter.2.cloned.1.call-done = f32[1,960,512]{1,2,0:T(8,128)} async-done(((f32[8,960,512]{1,2,0:T(8,128)}), f32[1,960,512]{1,2,0:T(8,128)}) %reduce-scatter.2.cloned.1.call-update) | async-done | bytes 1966096 | tf_op jit(solution)/shard_map/reduce_scatter | solution.py:181
  410.4 0.0 copy-done.1
  410.4 0.0 copy-done.4
  410.4 0.0 copy-done.6
  410.4 0.0 copy-start.2
  410.4 2.5 fusion.3
  412.9 0.0 copy-done.8
  412.9 0.0 copy-done.2
  412.9 0.5 fusion.7
  413.4 1.3 copy.12
  414.7 13.5 %psum.15 = f32[960]{0:T(1024)} all-reduce(f32[960]{0:T(1024)S(1)} %get-tuple-element.18), channel_id=1, replica_groups=mesh['dp'=4,'pp'=8] {'pp'}, use_global_device_ids=true, to_apply=%region_7.0 | all-reduce | flops 960 | bytes 7680 | tf_op jit(solution)/shard_map/psum | solution.py:183
  (2 shorter events, 0.0 us)
Async XLA Ops:
  7.2 56.6 %all-gather.2.cloned.1.call-start = ((), (), s32[]{:S(2)}) async-start(), calls=%async_computation.1 | async-start | bytes 9437184 | tf_op jit(solution)/shard_map/all_gather | solution.py:172
  8.7 3.5 copy-start
  9.5 0.9 copy-start.3
  9.7 0.6 copy-start.7
  10.3 0.6 copy-start.5
  12.3 398.1 %reduce-scatter.2.cloned.1.call-start = ((), (), s32[]{:S(2)}) async-start(), calls=%async_computation.2 | async-start | bytes 18874368 | tf_op jit(solution)/shard_map/reduce_scatter | solution.py:181
  12.4 16.4 %copy-start.9 = (s32[1,512]{1,0:T(1,128)S(1)}, s32[1,512]{1,0:T(1,128)}, u32[]{:S(2)}) copy-start(s32[1,512]{1,0:T(1,128)} %param.5) | copy-start | bytes 6148
  320.0 90.3 %copy-start.1 = (bf16[1,512,960]{2,1,0:T(8,128)(2,1)S(1)}, bf16[1,512,960]{2,1,0:T(8,128)(2,1)}, u32[]{:S(2)}) copy-start(bf16[1,512,960]{2,1,0:T(8,128)(2,1)} %copy-done) | copy-start | bytes 2949124
  320.1 90.3 %copy-start.4 = (f32[960]{0:T(1024)S(1)}, f32[960]{0:T(1024)}, u32[]{:S(2)}) copy-start(f32[960]{0:T(1024)} %copy-done.3) | copy-start | bytes 11524
  320.1 90.3 %copy-start.6 = (f32[512]{0:T(512)S(1)}, f32[512]{0:T(512)}, u32[]{:S(2)}) copy-start(f32[512]{0:T(512)} %copy-done.5) | copy-start | bytes 6148
  344.2 68.7 %copy-start.8 = (f32[512]{0:T(512)S(1)}, f32[512]{0:T(512)}, u32[]{:S(2)}) copy-start(f32[512]{0:T(512)} %copy-done.7) | copy-start | bytes 6148
  410.4 2.5 copy-start.2
Sparse Core Ops, SparseCore 0:
  12.4 51.2 all-gather.1
  320.2 90.1 reduce-scatter.1

commit v2 on v0

v2 whole, which is shorter than its diff:
```python
import functools
import math

import jax
import jax.numpy as jnp
from jax import lax
from jax.experimental import pallas as pl
from jax.experimental.pallas import tpu as pltpu
from jax.sharding import PartitionSpec as P

SOFT_CAP = 30.0
EPS = 1e-6
CAP_LOG2E = SOFT_CAP * math.log2(math.e)
FWD_TILE = 1536
BWD_TILE = 1024
SUB = 512
LANES = 128
VMEM_LIMIT = 66_000_000
AXIS = 'pp'
MESH_ID = pl.DeviceIdType.MESH
ANY = pl.BlockSpec(memory_space=pl.ANY)


def norm_cols(cols, gain):
    mean_sq = jnp.mean(cols * cols, axis=0, keepdims=True)
    return cols * lax.rsqrt(mean_sq + EPS) * (1.0 + gain[:, None])


def fold_lanes(x):
    return sum(x[:, i:i + LANES] for i in range(0, x.shape[1], LANES))


def spread(col, width):
    return jnp.concatenate([col] * (width // LANES), axis=1)


def row_to_col(row):
    return jnp.broadcast_to(row, (LANES, row.shape[1])).T


def enter(n):
    me = lax.axis_index(AXIS)
    barrier = pltpu.get_barrier_semaphore()
    for d in range(1, n):
        pl.semaphore_signal(barrier, inc=1, device_id={AXIS: lax.rem(me + d, n)}, device_id_type=MESH_ID)


def entered(n):
    pl.semaphore_wait(pltpu.get_barrier_semaphore(), n - 1)


def remote(src, dst, send_sem, recv_sem, peer):
    return pltpu.make_async_remote_copy(src_ref=src, dst_ref=dst, send_sem=send_sem, recv_sem=recv_sem,
                                        device_id={AXIS: peer}, device_id_type=MESH_ID)


def fwd_offset(step, n):
    half = (step + 1) // 2
    return lax.rem(jnp.where(lax.rem(step, 2) == 1, n - half, half), n)


def fwd_kernel(n, n_tiles, labels_hbm, own_hbm, w_hbm, tr_ref, tl_ref, n_hbm, labels_out, stats_out,
               w_ref, cols_ref, labels_ref, stats_ref, rows_ref, label_ref, exp_ref, hit_ref,
               w_sems, in_sems, out_sems, right_send, right_recv, left_send, left_recv,
               lab_send, lab_recv, stat_send, stat_recv):
    step, tile = pl.program_id(0), pl.program_id(1)
    me = lax.axis_index(AXIS)
    right, left = lax.rem(me + 1, n), lax.rem(me + n - 1, n)
    vocab = w_ref.shape[1]
    half = rows_ref.shape[0] // 2
    last = n - 1
    offset = fwd_offset(step, n)
    chunk = lax.rem(me + offset, n)

    def w_copy(i):
        cols = pl.ds(pl.multiple_of(i * FWD_TILE, FWD_TILE), FWD_TILE)
        return pltpu.make_async_copy(w_hbm.at[:, cols], w_ref.at[:, cols], w_sems.at[i])

    def hop(j, to_right):
        if to_right:
            src, dst, sends, recvs, peer = max(2 * j - 3, 0), 2 * j - 1, right_send, right_recv, right
        else:
            src, dst, sends, recvs, peer = 2 * j - 2, 2 * j, left_send, left_recv, left
        return remote(cols_ref.at[src], cols_ref.at[dst], sends.at[j], recvs.at[j], peer)

    def label_copy(d):
        return remote(labels_ref.at[me], labels_ref.at[me], lab_send.at[d], lab_recv.at[d], lax.rem(me + d, n))

    def label_arrival(d):
        src = lax.rem(me + n - d, n)
        return remote(labels_ref.at[src], labels_ref.at[src], lab_send.at[d], lab_recv.at[d], src)

    def stat_copy(k, d):
        slot = lax.rem(me + fwd_offset(k, n), n)
        return remote(stats_ref.at[me, slot], stats_ref.at[me, slot], stat_send.at[k, d], stat_recv.at[k, d],
                      lax.rem(me + d, n))

    def stat_arrival(k, d):
        src = lax.rem(me + n - d, n)
        slot = lax.rem(src + fwd_offset(k, n), n)
        return remote(stats_ref.at[src, slot], stats_ref.at[src, slot], stat_send.at[k, d], stat_recv.at[k, d], src)

    def n_copies(k):
        off = fwd_offset(k, n)
        to_r, to_l = lax.rem(2 * n - 1 - off, n), lax.rem(off + n - 1, n)
        return [pltpu.make_async_copy(cols_ref.at[k, :, 0:half], n_hbm.at[to_r, :, 0:half], out_sems.at[0, k]),
                pltpu.make_async_copy(cols_ref.at[k, :, half:2 * half], n_hbm.at[to_l, :, half:2 * half],
                                      out_sems.at[1, k])]

    right_hops, left_hops = n // 2, (n - 1) // 2

    @pl.when((step == 0) & (tile == 0))
    def _():
        enter(n)
        own = [pltpu.make_async_copy(own_hbm, cols_ref.at[0], in_sems.at[0]),
               pltpu.make_async_copy(labels_hbm, labels_ref.at[me], in_sems.at[1])]
        for copy in own:
            copy.start()
        for i in range(n_tiles):
            w_copy(i).start()
        for copy in own:
            copy.wait()
        entered(n)
        hop(1, True).start()
        hop(1, False).start()
        for d in range(1, n):
            label_copy(d).start()

    for j in range(1, right_hops + 1):
        @pl.when((step == 2 * j - 1) & (tile == 0))
        def _(j=j):
            hop(j, True).wait_recv()
            if j < right_hops:
                hop(j + 1, True).start()
            if j <= left_hops:
                hop(j, False).wait_recv()
            if j < left_hops:
                hop(j + 1, False).start()
            if j == 1:
                for d in range(1, n):
                    label_arrival(d).wait_recv()

    @pl.when((step > 0) & (tile == 0))
    def _():
        for d in range(1, n):
            stat_copy(step - 1, d).start()

    @pl.when(step == 0)
    def _():
        w_copy(tile).wait()

    @pl.when(tile == 0)
    def _():
        for copy in n_copies(step):
            copy.start()
        rows_ref[...] = cols_ref[step].T
        label_ref[...] = row_to_col(labels_ref[chunk]) - me * vocab
        exp_ref[...] = jnp.zeros_like(exp_ref)
        hit_ref[...] = jnp.zeros_like(hit_ref)

    rows = rows_ref[...]
    col0 = pl.multiple_of(tile * FWD_TILE, FWD_TILE)
    labels = label_ref[...] - col0
    iota = lax.broadcasted_iota(jnp.int32, (rows.shape[0], SUB), 1)
    exp_sum = exp_ref[...]
    label_sum = hit_ref[...]
    for s in range(FWD_TILE // SUB):
        w = w_ref[:, pl.ds(pl.multiple_of(col0 + s * SUB, SUB), SUB)]
        z = jnp.dot(rows, w, preferred_element_type=jnp.float32)
        t = jnp.tanh(z * (1.0 / SOFT_CAP))
        tr_ref[:, s * SUB:(s + 1) * SUB] = t[0:half]
        tl_ref[:, s * SUB:(s + 1) * SUB] = t[half:2 * half]
        exp_sum += fold_lanes(jnp.exp2(t * CAP_LOG2E))
        label_sum += fold_lanes(jnp.where(iota == spread(labels - s * SUB, SUB), t, 0.0))
    exp_ref[...] = exp_sum
    hit_ref[...] = label_sum

    @pl.when(tile == n_tiles - 1)
    def _():
        stats_ref[me, chunk, 0:1, :] = jnp.sum(exp_ref[...].T, axis=0, keepdims=True)
        stats_ref[me, chunk, 1:2, :] = jnp.sum(hit_ref[...].T, axis=0, keepdims=True)

    @pl.when((step == last) & (tile == n_tiles - 1))
    def _():
        labels_copy = pltpu.make_async_copy(labels_ref, labels_out, in_sems.at[1])
        labels_copy.start()
        for k in range(last):
            for d in range(1, n):
                stat_arrival(k, d).wait_recv()
                stat_copy(k, d).wait_send()
        for d in range(1, n):
            stat_copy(last, d).start()
        for j in range(1, right_hops + 1):
            hop(j, True).wait_send()
        for j in range(1, left_hops + 1):
            hop(j, False).wait_send()
        for d in range(1, n):
            label_copy(d).wait_send()
        for k in range(n):
            for copy in n_copies(k):
                copy.wait()
        labels_copy.wait()
        for d in range(1, n):
            stat_arrival(last, d).wait_recv()
        stats_out[...] = sum(stats_ref[i] for i in range(n))
        for d in range(1, n):
            stat_copy(last, d).wait_send()


def forward(n, normed, labels, table_t):
    width, chunk = normed.shape
    vocab = table_t.shape[1]
    tokens, half = n * chunk, chunk // 2
    n_tiles = vocab // FWD_TILE
    dma = pltpu.SemaphoreType.DMA

    def to_r(k, v):
        return lax.rem(2 * n - 1 - fwd_offset(k, n), n), 0, v

    def to_l(k, v):
        return lax.rem(fwd_offset(k, n) + n - 1, n), 0, v

    return pl.pallas_call(
        functools.partial(fwd_kernel, n, n_tiles),
        grid=(n, n_tiles),
        in_specs=[ANY, ANY, ANY],
        out_specs=[
            pl.BlockSpec((None, half, FWD_TILE), to_r),
            pl.BlockSpec((None, half, FWD_TILE), to_l),
            ANY,
            ANY,
            pl.BlockSpec((n, 2, chunk), lambda k, v: (0, 0, 0)),
        ],
        out_shape=[
            jax.ShapeDtypeStruct((n, half, vocab), jnp.float32),
            jax.ShapeDtypeStruct((n, half, vocab), jnp.float32),
            jax.ShapeDtypeStruct((n, width, chunk), normed.dtype),
            jax.ShapeDtypeStruct((n, 1, chunk), jnp.int32),
            jax.ShapeDtypeStruct((n, 2, chunk), jnp.float32),
        ],
        scratch_shapes=[
            pltpu.VMEM((width, vocab), table_t.dtype),
            pltpu.VMEM((n, width, chunk), normed.dtype),
            pltpu.VMEM((n, 1, chunk), jnp.int32),
            pltpu.VMEM((n, n, 2, chunk), jnp.float32),
            pltpu.VMEM((chunk, width), normed.dtype),
            pltpu.VMEM((chunk, LANES), jnp.int32),
            pltpu.VMEM((chunk, LANES), jnp.float32),
            pltpu.VMEM((chunk, LANES), jnp.float32),
            dma((n_tiles,)), dma((2,)), dma((2, n)), dma((n,)), dma((n,)), dma((n,)), dma((n,)),
            dma((n,)), dma((n,)), dma((n, n)), dma((n, n)),
        ],
        compiler_params=pltpu.CompilerParams(vmem_limit_bytes=VMEM_LIMIT, collective_id=0, has_side_effects=True),
        cost_estimate=pl.CostEstimate(flops=2 * tokens * vocab * width, transcendentals=2 * tokens * vocab,
                                      bytes_accessed=4 * tokens * vocab),
        name='head_fwd',
    )(labels, normed, table_t)


def bwd_kernel(n, n_tiles, total, labels_hbm, stats_hbm, hidden_hbm, gain_hbm, normed_ref, tr_ref, tl_ref, w_ref,
               dw_hbm, dh_hbm, dgain_ref,
               dw_ref, dn_ref, ring_ref, label_ref, scale_ref, labels_ref, stats_ref, hidden_ref, gain_ref, dh_ref, gains_ref,
               dw_sems, in_sems, ring_send, ring_recv, gain_send, gain_recv):
    step, tile = pl.program_id(0), pl.program_id(1)
    me = lax.axis_index(AXIS)
    right, left = lax.rem(me + 1, n), lax.rem(me + n - 1, n)
    vocab = dw_ref.shape[1]
    half = tr_ref.shape[0]
    last = n - 1
    from_r, from_l = lax.rem(me + 2 * n - 1 - step, n), lax.rem(me + 1 + step, n)
    col0 = pl.multiple_of(tile * BWD_TILE, BWD_TILE)
    tile_cols = pl.ds(col0, BWD_TILE)

    def pass_on(k, way):
        return remote(ring_ref.at[k, way], ring_ref.at[k + 1, way], ring_send.at[way, k], ring_recv.at[way, k],
                      (right, left)[way])

    def gain_copy(d):
        return remote(gains_ref.at[me], gains_ref.at[me], gain_send.at[d], gain_recv.at[d], lax.rem(me + d, n))

    def gain_arrival(d):
        src = lax.rem(me + n - d, n)
        return remote(gains_ref.at[src], gains_ref.at[src], gain_send.at[d], gain_recv.at[d], src)

    loads = [pltpu.make_async_copy(src, dst, in_sems.at[i]) for i, (src, dst) in enumerate(
        [(labels_hbm, labels_ref), (stats_hbm, stats_ref), (hidden_hbm, hidden_ref), (gain_hbm, gain_ref)])]

    @pl.when((step == 0) & (tile == 0))
    def _():
        enter(n)
        for copy in loads:
            copy.start()
        for copy in loads:
            copy.wait()
        entered(n)

    @pl.when((step > 0) & (tile == 0))
    def _():
        for way in range(2):
            pass_on(step - 1, way).start()

    @pl.when(tile == 0)
    def _():
        dn_ref[...] = jnp.zeros_like(dn_ref)
        labels = jnp.concatenate([labels_ref[from_r][:, 0:half], labels_ref[from_l][:, half:2 * half]], axis=1)
        label_ref[...] = row_to_col(labels) - me * vocab
        sums = jnp.concatenate([stats_ref[from_r, 0:1, 0:half], stats_ref[from_l, 0:1, half:2 * half]], axis=1)
        scale_ref[...] = row_to_col(1.0 / (sums * total))

    @pl.when(step == 0)
    def _():
        dw_ref[:, tile_cols] = jnp.zeros((dw_ref.shape[0], BWD_TILE), jnp.float32)

    normed = normed_ref[...]
    labels = label_ref[...] - col0
    scale = spread(scale_ref[...], SUB)
    iota = lax.broadcasted_iota(jnp.int32, (half, SUB), 1)
    dz = []
    for s in range(BWD_TILE // SUB):
        parts = []
        for h, t_ref in enumerate((tr_ref, tl_ref)):
            rows = slice(h * half, (h + 1) * half)
            t = t_ref[:, s * SUB:(s + 1) * SUB]
            p = jnp.exp2(t * CAP_LOG2E) * scale[rows]
            dc = jnp.where(iota == spread(labels[rows] - s * SUB, SUB), p - 1.0 / total, p)
            parts.append((dc * (1.0 - t * t)).astype(jnp.bfloat16))
        dz.append(jnp.concatenate(parts, axis=0))
        cols = pl.ds(pl.multiple_of(col0 + s * SUB, SUB), SUB)
        dw_ref[:, cols] += jnp.dot(normed, dz[-1], preferred_element_type=jnp.float32)
    dz = jnp.concatenate(dz, axis=1)
    dn_ref[...] += lax.dot_general(w_ref[...], dz, (((1,), (1,)), ((), ())), preferred_element_type=jnp.float32)

    @pl.when(step == last)
    def _():
        pltpu.make_async_copy(dw_ref.at[:, tile_cols], dw_hbm.at[:, tile_cols], dw_sems.at[tile]).start()

    @pl.when((step == 0) & (tile == n_tiles - 1))
    def _():
        ring_ref[0, 0] = dn_ref[:, 0:half]
        ring_ref[0, 1] = dn_ref[:, half:2 * half]

    @pl.when((step > 0) & (tile == n_tiles - 1))
    def _():
        for way in range(2):
            pass_on(step - 1, way).wait_recv()
            ring_ref[step, way] += dn_ref[:, way * half:(way + 1) * half]

    @pl.when((step == last) & (tile == n_tiles - 1))
    def _():
        width = hidden_ref.shape[0]
        gain = 1.0 + gain_ref[...]
        folds = []
        for way in range(2):
            cols = slice(way * half, (way + 1) * half)
            x = hidden_ref[:, cols].astype(jnp.float32)
            dn = ring_ref[last, way]
            r = lax.rsqrt(jnp.mean(x * x, axis=0, keepdims=True) + EPS)
            folds.append(fold_lanes(dn * x * r))
            dy = dn * gain
            dot = jnp.sum(dy * x, axis=0, keepdims=True)
            dh_ref[:, cols] = (dy * r - x * (r * r * r * dot * (1.0 / width))).astype(dh_ref.dtype)
        gains_ref[me] = jnp.sum((folds[0] + folds[1]).T, axis=0, keepdims=True)
        dh_copy = pltpu.make_async_copy(dh_ref, dh_hbm, in_sems.at[0])
        dh_copy.start()
        for k in range(last):
            for way in range(2):
                pass_on(k, way).wait_send()
        for d in range(1, n):
            gain_copy(d).start()
        for i in range(n_tiles):
            cols = pl.ds(i * BWD_TILE, BWD_TILE)
            pltpu.make_async_copy(dw_ref.at[:, cols], dw_hbm.at[:, cols], dw_sems.at[i]).wait()
        dh_copy.wait()
        for d in range(1, n):
            gain_arrival(d).wait_recv()
        dgain_ref[...] = sum(gains_ref[i] for i in range(n))
        for d in range(1, n):
            gain_copy(d).wait_send()


def backward(n, labels, stats, hidden_t, gain, normed, t_r, t_l, table_t):
    _, width, chunk = normed.shape
    vocab = table_t.shape[1]
    tokens, half = n * chunk, chunk // 2
    n_tiles = vocab // BWD_TILE
    dma = pltpu.SemaphoreType.DMA
    return pl.pallas_call(
        functools.partial(bwd_kernel, n, n_tiles, tokens),
        grid=(n, n_tiles),
        in_specs=[
            ANY, ANY, ANY, ANY,
            pl.BlockSpec((None, width, chunk), lambda s, v: (s, 0, 0)),
            pl.BlockSpec((None, half, BWD_TILE), lambda s, v: (s, 0, v)),
            pl.BlockSpec((None, half, BWD_TILE), lambda s, v: (s, 0, v)),
            pl.BlockSpec((width, BWD_TILE), lambda s, v: (0, v)),
        ],
        out_specs=[ANY, ANY, pl.BlockSpec((1, width), lambda s, v: (0, 0))],
        out_shape=[
            jax.ShapeDtypeStruct((width, vocab), jnp.float32),
            jax.ShapeDtypeStruct((width, chunk), jnp.bfloat16),
            jax.ShapeDtypeStruct((1, width), jnp.float32),
        ],
        scratch_shapes=[
            pltpu.VMEM((width, vocab), jnp.float32),
            pltpu.VMEM((width, chunk), jnp.float32),
            pltpu.VMEM((n, 2, width, half), jnp.float32),
            pltpu.VMEM((chunk, LANES), jnp.int32),
            pltpu.VMEM((chunk, LANES), jnp.float32),
            pltpu.VMEM((n, 1, chunk), jnp.int32),
            pltpu.VMEM((n, 2, chunk), jnp.float32),
            pltpu.VMEM((width, chunk), jnp.bfloat16),
            pltpu.VMEM((width, 1), jnp.float32),
            pltpu.VMEM((width, chunk), jnp.bfloat16),
            pltpu.VMEM((n, 1, width), jnp.float32),
            dma((n_tiles,)), dma((4,)), dma((2, n)), dma((2, n)), dma((n,)), dma((n,)),
        ],
        compiler_params=pltpu.CompilerParams(vmem_limit_bytes=VMEM_LIMIT, collective_id=1, has_side_effects=True),
        cost_estimate=pl.CostEstimate(flops=4 * tokens * vocab * width, transcendentals=tokens * vocab,
                                      bytes_accessed=4 * tokens * vocab),
        name='head_bwd',
    )(labels, stats, hidden_t, gain, normed, t_r, t_l, table_t)


def solution(mesh):
    n = mesh.shape[AXIS]

    def local_fn(hidden, labels, gamma, table):
        mb_dev, seq_len, width = hidden.shape
        rank = lax.axis_index(AXIS)
        own = mb_dev * seq_len
        hidden_t = hidden.reshape(own, width).T
        normed = norm_cols(hidden_t.astype(jnp.float32), gamma).astype(jnp.bfloat16)
        table_t = table.T
        t_r, t_l, all_normed, all_labels, stats = forward(n, normed, labels.reshape(1, own), table_t)
        all_loss = jnp.log(stats[:, 0]) - SOFT_CAP * stats[:, 1]
        grad_table_t, grad_hidden_t, grad_gain = backward(n, all_labels, stats, hidden_t, gamma[:, None], all_normed,
                                                          t_r, t_l, table_t)
        own_loss = lax.dynamic_slice_in_dim(all_loss, rank, 1, axis=0).reshape(mb_dev, seq_len)
        mean_loss = jnp.reshape(jnp.mean(all_loss), (1,))
        grad_hidden = grad_hidden_t.T.reshape(mb_dev, seq_len, width)
        return own_loss, grad_hidden, mean_loss, grad_table_t.T, grad_gain[0]

    token_spec = P(('dp', 'pp'))
    return jax.shard_map(local_fn, mesh=mesh,
                         in_specs=(token_spec, token_spec, P(), P('pp')),
                         out_specs=(token_spec, token_spec, P('dp'), token_spec, P('dp')),
                         check_vma=False)
```

time: 872 us -> 264 us (0.30)
  matrix products: 428 us -> 0 us
  Pallas kernels: 0 us -> 235 us
  blocking collectives: 228 us -> 0 us
  waiting for transfers between devices: 115 us -> 0 us
  other arithmetic: 80.9 us -> 5.24 us
  local copies, waits for them, and re-layouts: 2.39 us -> 21 us
  between operations: 15.9 us -> 2.45 us
    dot_general x24 -> x0, matrix products: 428 us -> none  [the longest x8 189 us: micro_step(): lax.dot_general(grad_logits, block, (((0,), (0,)), ((), ())), preferred_e...]
    pallas_call x0 -> x2, Pallas kernels: none -> 235 us  [the longest x1 134 us: backward(): pl.pallas_call(functools.partial(bwd_kernel, n, n_tiles, tokens), grid=(n...]
    psum x9 -> x0, blocking collectives: 114 us -> none  [the longest x8 101 us: micro_step(): group_stats = lax.psum(local_stats, 'pp')]
    pmax x8 -> x0, blocking collectives: 99.3 us -> none  [micro_step(): row_max = lax.pmax(jnp.max(capped, axis=1), 'pp')]
    reduce_scatter x1 -> x0, waiting for transfers between devices: 81.2 us -> none  [local_fn(): own_dn = lax.psum_scatter(all_dn, 'pp', scatter_dimension=0, tiled=True)]
    reduce_sum x10 -> x1, other arithmetic: 73.9 us -> 1.46 us  [norm_cols(): mean_sq = jnp.mean(cols * cols, axis=0, keepdims=True)]
    all_gather x1 -> x0, waiting for transfers between devices: 34 us -> none  [local_fn(): all_normed = lax.all_gather(normed, 'pp', axis=0, tiled=True)]
    unnamed x15 -> x9, local copies, waits for them, and re-layouts: 1.2 us -> 19.4 us
  transfers between devices with their start and end apart: 2 -> 0, of which waited for: 2 -> 0; matrix products, arithmetic and copies ran while one was open for 0% -> 0% of each run, Pallas kernels for 0% -> 0%
where the time goes in v2:
time: 264 us
  Pallas kernels  235 us (89%)
  local copies, waits for them, and re-layouts  21 us (8%)
  other arithmetic  5.24 us (2%)
    pallas_call x1, Pallas kernels, backward(): pl.pallas_call(functools.partial(bwd_kernel, n, n_tiles, tokens), grid=(n...  134 us
    pallas_call x1, Pallas kernels, forward(): pl.pallas_call(functools.partial(fwd_kernel, n, n_tiles), grid=(n, n_tile...  101 us
    unnamed x9, local copies, waits for them, and re-layouts  19.4 us

profile of v2, /device:TPU:81, one launch (start us, length us, event | category | flops | bytes accessed | tf_op | source)
XLA Modules:
  0.0 263.5 jit_solution(11983929741020265170)
XLA Ops:
  0.6 1.5 fusion
  2.1 0.7 broadcast_add_fusion
  2.8 2.4 fusion.2.own_hbm
  5.2 0.0 copy-start.1
  5.2 100.9 %head_fwd.1 = (f32[8,256,6144]{2,1,0:T(8,128)}, f32[8,256,6144]{2,1,0:T(8,128)}, bf16[8,960,512]{2,1,0:T(8,128)(2,1)}, s32[8,1,512]{2,1,0:T(1,128)}, f32[8,2,512]{2,1,0:T(2,128)}) custom-call(s32[1,512]{1,0:T(1,128)} %labels_hbm.1, bf16[960,512]{1,0:T(8,128)(2,1)} %fusion.2.own_hbm, bf16[960,6144]{1,0:T(8,128)(2,1)} %bitcast.20), custom_call_target="tpu_custom_call" | custom-call | flops 48318382080 | bytes 100663296 | tf_op jit(solution)/shard_map/head_fwd/pallas_call | solution.py:223
  106.1 0.0 copy-done.1
  106.1 1.0 copy.9.gain_hbm
  107.1 0.0 copy-start
  107.1 134.0 %head_bwd.1 = (f32[960,6144]{1,0:T(8,128)}, bf16[960,512]{1,0:T(8,128)(2,1)}, f32[1,960]{1,0:T(1,128)}) custom-call(s32[8,1,512]{2,1,0:T(1,128)} %get-tuple-element.14.labels_hbm, f32[8,2,512]{2,1,0:T(2,128)} %get-tuple-element.13.stats_hbm, bf16[960,512]{1,0:T(8,128)(2,1)} %bitcast.16, f32[960,1]{1,0:T(8,128)} %copy.9.gain_hbm, ...), custom_call_target="tpu_custom_call" | custom-call | flops 96636764160 | bytes 100663296 | tf_op jit(solution)/shard_map/head_bwd/pallas_call | solution.py:387
  241.1 0.0 copy-done
  241.1 0.6 fusion.3
  241.8 0.6 dynamic-slice_bitcast_fusion
  243.0 2.2 copy.13
  245.2 0.0 copy-start.2
  245.2 16.6 %copy.14 = f32[6144,960]{0,1:T(8,128)} copy(f32[6144,960]{0,1:T(8,128)} %bitcast.15) | data formatting | bytes 47185920
  261.8 0.0 copy-done.2
  261.8 0.6 copy.15
  (1 shorter events, 0.0 us)
Async XLA Ops:
  5.2 100.9 %copy-start.1 = (f32[960]{0:T(1024)S(1)}, f32[960]{0:T(1024)}, u32[]{:S(2)}) copy-start(f32[960]{0:T(1024)} %param.6) | copy-start | bytes 11524
  107.1 134.0 %copy-start = (f32[8,2,512]{2,1,0:T(2,128)S(1)}, f32[8,2,512]{2,1,0:T(2,128)}, u32[]{:S(2)}) copy-start(f32[8,2,512]{2,1,0:T(2,128)} %get-tuple-element.13.stats_hbm) | copy-start | bytes 98308
  245.2 16.6 %copy-start.2 = (f32[1,960]{1,0:T(1,128)S(1)}, f32[1,960]{1,0:T(1,128)}, u32[]{:S(2)}) copy-start(f32[1,960]{1,0:T(1,128)} %get-tuple-element.20) | copy-start | bytes 11524

commit v3 on v2

--- a/solution.py
+++ b/solution.py
@@ -11,8 +11,9 @@
 SOFT_CAP = 30.0
 EPS = 1e-6
 CAP_LOG2E = SOFT_CAP * math.log2(math.e)
-FWD_TILE = 1536
-BWD_TILE = 1024
+FWD_TILE = 3072
+BWD_TILE = 2048
+LATE_TILES = 1
 SUB = 512
 LANES = 128
 VMEM_LIMIT = 66_000_000
@@ -21,11 +22,6 @@
 ANY = pl.BlockSpec(memory_space=pl.ANY)
 
 
-def norm_cols(cols, gain):
-    mean_sq = jnp.mean(cols * cols, axis=0, keepdims=True)
-    return cols * lax.rsqrt(mean_sq + EPS) * (1.0 + gain[:, None])
-
-
 def fold_lanes(x):
     return sum(x[:, i:i + LANES] for i in range(0, x.shape[1], LANES))
 
@@ -59,8 +55,8 @@
     return lax.rem(jnp.where(lax.rem(step, 2) == 1, n - half, half), n)
 
 
-def fwd_kernel(n, n_tiles, labels_hbm, own_hbm, w_hbm, tr_ref, tl_ref, n_hbm, labels_out, stats_out,
-               w_ref, cols_ref, labels_ref, stats_ref, rows_ref, label_ref, exp_ref, hit_ref,
+def fwd_kernel(n, n_tiles, labels_hbm, hidden_hbm, gain_hbm, w_hbm, tr_ref, tl_ref, n_hbm, labels_out, stats_out,
+               w_ref, cols_ref, labels_ref, stats_ref, rows_ref, label_ref, exp_ref, hit_ref, hidden_ref, gain_ref,
                w_sems, in_sems, out_sems, right_send, right_recv, left_send, left_recv,
                lab_send, lab_recv, stat_send, stat_recv):
     step, tile = pl.program_id(0), pl.program_id(1)
@@ -112,14 +108,18 @@
     @pl.when((step == 0) & (tile == 0))
     def _():
         enter(n)
-        own = [pltpu.make_async_copy(own_hbm, cols_ref.at[0], in_sems.at[0]),
-               pltpu.make_async_copy(labels_hbm, labels_ref.at[me], in_sems.at[1])]
+        own = [pltpu.make_async_copy(hidden_hbm, hidden_ref, in_sems.at[0]),
+               pltpu.make_async_copy(labels_hbm, labels_ref.at[me], in_sems.at[1]),
+               pltpu.make_async_copy(gain_hbm, gain_ref, in_sems.at[2])]
         for copy in own:
             copy.start()
         for i in range(n_tiles):
             w_copy(i).start()
         for copy in own:
             copy.wait()
+        x = hidden_ref[...].astype(jnp.float32)
+        scale = lax.rsqrt(jnp.mean(x * x, axis=0, keepdims=True) + EPS)
+        cols_ref[0] = (x * scale * (1.0 + gain_ref[...])).astype(cols_ref.dtype)
         entered(n)
         hop(1, True).start()
         hop(1, False).start()
@@ -162,18 +162,16 @@
     col0 = pl.multiple_of(tile * FWD_TILE, FWD_TILE)
     labels = label_ref[...] - col0
     iota = lax.broadcasted_iota(jnp.int32, (rows.shape[0], SUB), 1)
-    exp_sum = exp_ref[...]
-    label_sum = hit_ref[...]
     for s in range(FWD_TILE // SUB):
         w = w_ref[:, pl.ds(pl.multiple_of(col0 + s * SUB, SUB), SUB)]
-        z = jnp.dot(rows, w, preferred_element_type=jnp.float32)
-        t = jnp.tanh(z * (1.0 / SOFT_CAP))
-        tr_ref[:, s * SUB:(s + 1) * SUB] = t[0:half]
-        tl_ref[:, s * SUB:(s + 1) * SUB] = t[half:2 * half]
-        exp_sum += fold_lanes(jnp.exp2(t * CAP_LOG2E))
-        label_sum += fold_lanes(jnp.where(iota == spread(labels - s * SUB, SUB), t, 0.0))
-    exp_ref[...] = exp_sum
-    hit_ref[...] = label_sum
+        for r in range(0, 2 * half, LANES):
+            row = slice(r, r + LANES)
+            z = jnp.dot(rows[row], w, preferred_element_type=jnp.float32)
+            t = jnp.tanh(z * (1.0 / SOFT_CAP))
+            out = tr_ref if r < half else tl_ref
+            out[r % half:r % half + LANES, s * SUB:(s + 1) * SUB] = t
+            exp_ref[row, :] += fold_lanes(jnp.exp2(t * CAP_LOG2E))
+            hit_ref[row, :] += fold_lanes(jnp.where(iota[row] == spread(labels[row] - s * SUB, SUB), t, 0.0))
 
     @pl.when(tile == n_tiles - 1)
     def _():
@@ -207,8 +205,8 @@
             stat_copy(last, d).wait_send()
 
 
-def forward(n, normed, labels, table_t):
-    width, chunk = normed.shape
+def forward(n, hidden_t, gain, labels, table_t):
+    width, chunk = hidden_t.shape
     vocab = table_t.shape[1]
     tokens, half = n * chunk, chunk // 2
     n_tiles = vocab // FWD_TILE
@@ -223,7 +221,7 @@
     return pl.pallas_call(
         functools.partial(fwd_kernel, n, n_tiles),
         grid=(n, n_tiles),
-        in_specs=[ANY, ANY, ANY],
+        in_specs=[ANY, ANY, ANY, ANY],
         out_specs=[
             pl.BlockSpec((None, half, FWD_TILE), to_r),
             pl.BlockSpec((None, half, FWD_TILE), to_l),
@@ -234,37 +232,40 @@
         out_shape=[
             jax.ShapeDtypeStruct((n, half, vocab), jnp.float32),
             jax.ShapeDtypeStruct((n, half, vocab), jnp.float32),
-            jax.ShapeDtypeStruct((n, width, chunk), normed.dtype),
+            jax.ShapeDtypeStruct((n, width, chunk), jnp.bfloat16),
             jax.ShapeDtypeStruct((n, 1, chunk), jnp.int32),
             jax.ShapeDtypeStruct((n, 2, chunk), jnp.float32),
         ],
         scratch_shapes=[
             pltpu.VMEM((width, vocab), table_t.dtype),
-            pltpu.VMEM((n, width, chunk), normed.dtype),
+            pltpu.VMEM((n, width, chunk), jnp.bfloat16),
             pltpu.VMEM((n, 1, chunk), jnp.int32),
             pltpu.VMEM((n, n, 2, chunk), jnp.float32),
-            pltpu.VMEM((chunk, width), normed.dtype),
+            pltpu.VMEM((chunk, width), jnp.bfloat16),
             pltpu.VMEM((chunk, LANES), jnp.int32),
             pltpu.VMEM((chunk, LANES), jnp.float32),
             pltpu.VMEM((chunk, LANES), jnp.float32),
-            dma((n_tiles,)), dma((2,)), dma((2, n)), dma((n,)), dma((n,)), dma((n,)), dma((n,)),
+            pltpu.VMEM((width, chunk), hidden_t.dtype),
+            pltpu.VMEM((width, 1), jnp.float32),
+            dma((n_tiles,)), dma((3,)), dma((2, n)), dma((n,)), dma((n,)), dma((n,)), dma((n,)),
             dma((n,)), dma((n,)), dma((n, n)), dma((n, n)),
         ],
         compiler_params=pltpu.CompilerParams(vmem_limit_bytes=VMEM_LIMIT, collective_id=0, has_side_effects=True),
         cost_estimate=pl.CostEstimate(flops=2 * tokens * vocab * width, transcendentals=2 * tokens * vocab,
                                       bytes_accessed=4 * tokens * vocab),
         name='head_fwd',
-    )(labels, normed, table_t)
+    )(labels, hidden_t, gain, table_t)
 
 
 def bwd_kernel(n, n_tiles, total, labels_hbm, stats_hbm, hidden_hbm, gain_hbm, normed_ref, tr_ref, tl_ref, w_ref,
-               dw_hbm, dh_hbm, dgain_ref,
+               dw_hbm, dz_ref, dh_hbm, dgain_ref,
                dw_ref, dn_ref, ring_ref, label_ref, scale_ref, labels_ref, stats_ref, hidden_ref, gain_ref, dh_ref, gains_ref,
                dw_sems, in_sems, ring_send, ring_recv, gain_send, gain_recv):
     step, tile = pl.program_id(0), pl.program_id(1)
     me = lax.axis_index(AXIS)
     right, left = lax.rem(me + 1, n), lax.rem(me + n - 1, n)
-    vocab = dw_ref.shape[1]
+    vocab = n_tiles * BWD_TILE
+    n_early = n_tiles - LATE_TILES
     half = tr_ref.shape[0]
     last = n - 1
     from_r, from_l = lax.rem(me + 2 * n - 1 - step, n), lax.rem(me + 1 + step, n)
@@ -292,6 +293,9 @@
             copy.start()
         for copy in loads:
             copy.wait()
+
+    @pl.when((step == 1) & (tile == 0))
+    def _():
         entered(n)
 
     @pl.when((step > 0) & (tile == 0))
@@ -307,32 +311,43 @@
         sums = jnp.concatenate([stats_ref[from_r, 0:1, 0:half], stats_ref[from_l, 0:1, half:2 * half]], axis=1)
         scale_ref[...] = row_to_col(1.0 / (sums * total))
 
-    @pl.when(step == 0)
-    def _():
-        dw_ref[:, tile_cols] = jnp.zeros((dw_ref.shape[0], BWD_TILE), jnp.float32)
-
-    normed = normed_ref[...]
-    labels = label_ref[...] - col0
-    scale = spread(scale_ref[...], SUB)
-    iota = lax.broadcasted_iota(jnp.int32, (half, SUB), 1)
-    dz = []
-    for s in range(BWD_TILE // SUB):
+    def logit_grads(sub):
+        labels = label_ref[...] - (col0 + sub * SUB)
+        iota = lax.broadcasted_iota(jnp.int32, (half, SUB), 1)
         parts = []
         for h, t_ref in enumerate((tr_ref, tl_ref)):
             rows = slice(h * half, (h + 1) * half)
-            t = t_ref[:, s * SUB:(s + 1) * SUB]
-            p = jnp.exp2(t * CAP_LOG2E) * scale[rows]
-            dc = jnp.where(iota == spread(labels[rows] - s * SUB, SUB), p - 1.0 / total, p)
+            t = t_ref[:, sub * SUB:(sub + 1) * SUB]
+            p = jnp.exp2(t * CAP_LOG2E) * spread(scale_ref[rows, :], SUB)
+            dc = jnp.where(iota == spread(labels[rows], SUB), p - 1.0 / total, p)
             parts.append((dc * (1.0 - t * t)).astype(jnp.bfloat16))
-        dz.append(jnp.concatenate(parts, axis=0))
-        cols = pl.ds(pl.multiple_of(col0 + s * SUB, SUB), SUB)
-        dw_ref[:, cols] += jnp.dot(normed, dz[-1], preferred_element_type=jnp.float32)
-    dz = jnp.concatenate(dz, axis=1)
-    dn_ref[...] += lax.dot_general(w_ref[...], dz, (((1,), (1,)), ((), ())), preferred_element_type=jnp.float32)
-
-    @pl.when(step == last)
-    def _():
-        pltpu.make_async_copy(dw_ref.at[:, tile_cols], dw_hbm.at[:, tile_cols], dw_sems.at[tile]).start()
+        return jnp.concatenate(parts, axis=0)
+
+    def add_dn(dz):
+        dn_ref[...] += lax.dot_general(w_ref[...], dz, (((1,), (1,)), ((), ())), preferred_element_type=jnp.float32)
+
+    @pl.when(tile < n_early)
+    def _():
+        @pl.when(step == 0)
+        def _():
+            dw_ref[:, tile_cols] = jnp.zeros((dw_ref.shape[0], BWD_TILE), jnp.float32)
+
+        dz = []
+        for sub in range(BWD_TILE // SUB):
+            dz.append(logit_grads(sub))
+            cols = pl.ds(pl.multiple_of(col0 + sub * SUB, SUB), SUB)
+            dw_ref[:, cols] += jnp.dot(normed_ref[...], dz[-1], preferred_element_type=jnp.float32)
+        add_dn(jnp.concatenate(dz, axis=1))
+
+        @pl.when(step == last)
+        def _():
+            pltpu.make_async_copy(dw_ref.at[:, tile_cols], dw_hbm.at[:, tile_cols], dw_sems.at[tile]).start()
+
+    @pl.when(tile >= n_early)
+    def _():
+        dz = jnp.concatenate([logit_grads(sub) for sub in range(BWD_TILE // SUB)], axis=1)
+        dz_ref[...] = dz
+        add_dn(dz)
 
     @pl.when((step == 0) & (tile == n_tiles - 1))
     def _():
@@ -367,7 +382,7 @@
                 pass_on(k, way).wait_send()
         for d in range(1, n):
             gain_copy(d).start()
-        for i in range(n_tiles):
+        for i in range(n_early):
             cols = pl.ds(i * BWD_TILE, BWD_TILE)
             pltpu.make_async_copy(dw_ref.at[:, cols], dw_hbm.at[:, cols], dw_sems.at[i]).wait()
         dh_copy.wait()
@@ -383,6 +398,8 @@
     vocab = table_t.shape[1]
     tokens, half = n * chunk, chunk // 2
     n_tiles = vocab // BWD_TILE
+    n_early = n_tiles - LATE_TILES
+    early = n_early * BWD_TILE
     dma = pltpu.SemaphoreType.DMA
     return pl.pallas_call(
         functools.partial(bwd_kernel, n, n_tiles, tokens),
@@ -394,14 +411,20 @@
             pl.BlockSpec((None, half, BWD_TILE), lambda s, v: (s, 0, v)),
             pl.BlockSpec((width, BWD_TILE), lambda s, v: (0, v)),
         ],
-        out_specs=[ANY, ANY, pl.BlockSpec((1, width), lambda s, v: (0, 0))],
+        out_specs=[
+            ANY,
+            pl.BlockSpec((None, chunk, BWD_TILE), lambda s, v: (s, 0, jnp.maximum(v - n_early, 0))),
+            ANY,
+            pl.BlockSpec((1, width), lambda s, v: (0, 0)),
+        ],
         out_shape=[
-            jax.ShapeDtypeStruct((width, vocab), jnp.float32),
+            jax.ShapeDtypeStruct((width, early), jnp.float32),
+            jax.ShapeDtypeStruct((n, chunk, vocab - early), jnp.bfloat16),
             jax.ShapeDtypeStruct((width, chunk), jnp.bfloat16),
             jax.ShapeDtypeStruct((1, width), jnp.float32),
         ],
         scratch_shapes=[
-            pltpu.VMEM((width, vocab), jnp.float32),
+            pltpu.VMEM((width, early), jnp.float32),
             pltpu.VMEM((width, chunk), jnp.float32),
             pltpu.VMEM((n, 2, width, half), jnp.float32),
             pltpu.VMEM((chunk, LANES), jnp.int32),
@@ -412,7 +435,7 @@
             pltpu.VMEM((width, 1), jnp.float32),
             pltpu.VMEM((width, chunk), jnp.bfloat16),
             pltpu.VMEM((n, 1, width), jnp.float32),
-            dma((n_tiles,)), dma((4,)), dma((2, n)), dma((2, n)), dma((n,)), dma((n,)),
+            dma((n_early,)), dma((4,)), dma((2, n)), dma((2, n)), dma((n,)), dma((n,)),
         ],
         compiler_params=pltpu.CompilerParams(vmem_limit_bytes=VMEM_LIMIT, collective_id=1, has_side_effects=True),
         cost_estimate=pl.CostEstimate(flops=4 * tokens * vocab * width, transcendentals=tokens * vocab,
@@ -421,6 +444,83 @@
     )(labels, stats, hidden_t, gain, normed, t_r, t_l, table_t)
 
 
+def late_kernel(n, early_hbm, normed_hbm, dz_hbm, dw_hbm, early_ref, normed_ref, dz_ref, dw_ref,
+                early_in, early_out, normed_sems, dz_sems, out_sems):
+    early, late = early_ref.shape[1], dw_ref.shape[1]
+    parts = late // SUB
+    piece = early // parts
+
+    def cols_of(i, size):
+        return pl.ds(pl.multiple_of(i * size, size), size)
+
+    def fetch(i):
+        return pltpu.make_async_copy(early_hbm.at[:, cols_of(i, piece)], early_ref.at[:, cols_of(i, piece)], early_in.at[i])
+
+    def put(i):
+        return pltpu.make_async_copy(early_ref.at[:, cols_of(i, piece)], dw_hbm.at[:, cols_of(i, piece)], early_out.at[i])
+
+    def result(i):
+        to = pl.ds(pl.multiple_of(early + i * SUB, SUB), SUB)
+        return pltpu.make_async_copy(dw_ref.at[:, cols_of(i, SUB)], dw_hbm.at[:, to], out_sems.at[i])
+
+    operands = [(pltpu.make_async_copy(normed_hbm.at[s], normed_ref.at[s], normed_sems.at[s]),
+                 pltpu.make_async_copy(dz_hbm.at[s], dz_ref.at[s], dz_sems.at[s])) for s in range(n)]
+    for pair in operands:
+        for copy in pair:
+            copy.start()
+    for i in range(parts):
+        fetch(i).start()
+
+    def part(i, carry):
+        cols = cols_of(i, SUB)
+        for lo, hi in ((0, n // 4), (n // 4, n)):
+            @pl.when(i == 0)
+            def _(lo=lo, hi=hi):
+                for pair in operands[lo:hi]:
+                    for copy in pair:
+                        copy.wait()
+
+            acc = sum(jnp.dot(normed_ref[s], dz_ref[s, :, cols], preferred_element_type=jnp.float32)
+                      for s in range(lo, hi))
+            if lo == 0:
+                dw_ref[:, cols] = acc
+            else:
+                dw_ref[:, cols] += acc
+        result(i).start()
+        fetch(i).wait()
+        put(i).start()
+        return carry
+
+    lax.fori_loop(0, parts, part, 0)
+    for i in range(parts):
+        put(i).wait()
+        result(i).wait()
+
+
+def late(early_dw, normed, dz):
+    n, width, chunk = normed.shape
+    early, late_cols = early_dw.shape[1], dz.shape[2]
+    vocab, parts = early + late_cols, late_cols // SUB
+    dma = pltpu.SemaphoreType.DMA
+    return pl.pallas_call(
+        functools.partial(late_kernel, n),
+        in_specs=[ANY, ANY, ANY],
+        out_specs=ANY,
+        out_shape=jax.ShapeDtypeStruct((width, vocab), jnp.float32),
+        scratch_shapes=[
+            pltpu.VMEM((width, early), jnp.float32),
+            pltpu.VMEM((n, width, chunk), normed.dtype),
+            pltpu.VMEM((n, chunk, late_cols), dz.dtype),
+            pltpu.VMEM((width, late_cols), jnp.float32),
+            dma((parts,)), dma((parts,)), dma((n,)), dma((n,)), dma((parts,)),
+        ],
+        compiler_params=pltpu.CompilerParams(vmem_limit_bytes=VMEM_LIMIT),
+        cost_estimate=pl.CostEstimate(flops=2 * n * chunk * late_cols * width, transcendentals=0,
+                                      bytes_accessed=8 * width * vocab),
+        name='head_dw',
+    )(early_dw, normed, dz)
+
+
 def solution(mesh):
     n = mesh.shape[AXIS]
 
@@ -429,12 +529,12 @@
         rank = lax.axis_index(AXIS)
         own = mb_dev * seq_len
         hidden_t = hidden.reshape(own, width).T
-        normed = norm_cols(hidden_t.astype(jnp.float32), gamma).astype(jnp.bfloat16)
+        gain = gamma[:, None]
         table_t = table.T
-        t_r, t_l, all_normed, all_labels, stats = forward(n, normed, labels.reshape(1, own), table_t)
+        t_r, t_l, all_normed, all_labels, stats = forward(n, hidden_t, gain, labels.reshape(1, own), table_t)
         all_loss = jnp.log(stats[:, 0]) - SOFT_CAP * stats[:, 1]
-        grad_table_t, grad_hidden_t, grad_gain = backward(n, all_labels, stats, hidden_t, gamma[:, None], all_normed,
-                                                          t_r, t_l, table_t)
+        early_dw, dz, grad_hidden_t, grad_gain = backward(n, all_labels, stats, hidden_t, gain, all_normed, t_r, t_l, table_t)
+        grad_table_t = late(early_dw, all_normed, dz)
         own_loss = lax.dynamic_slice_in_dim(all_loss, rank, 1, axis=0).reshape(mb_dev, seq_len)
         mean_loss = jnp.reshape(jnp.mean(all_loss), (1,))
         grad_hidden = grad_hidden_t.T.reshape(mb_dev, seq_len, width)

time: 264 us -> 250 us (0.947)
  local copies, waits for them, and re-layouts: 21 us -> 3.81 us
  Pallas kernels: 235 us -> 243 us
  other arithmetic: 5.24 us -> 0.64 us
    pallas_call x0 -> x1, Pallas kernels: none -> 30.3 us  [late(): pl.pallas_call(functools.partial(late_kernel, n), in_specs=[ANY, ANY, ANY...]
    unnamed x9 -> x8, local copies, waits for them, and re-layouts: 19.4 us -> 1.55 us
    pallas_call x1, Pallas kernels: 134 us -> 122 us  [backward(): pl.pallas_call(functools.partial(bwd_kernel, n, n_tiles, tokens), grid=(n...]
    pallas_call x1, Pallas kernels: 101 us -> 90.5 us  [forward(): pl.pallas_call(functools.partial(fwd_kernel, n, n_tiles), grid=(n, n_tile...]
where the time goes in v3:
time: 250 us
  Pallas kernels  243 us (97%)
  local copies, waits for them, and re-layouts  3.81 us (2%)
    pallas_call x1, Pallas kernels, backward(): pl.pallas_call(functools.partial(bwd_kernel, n, n_tiles, tokens), grid=(n...  122 us
    pallas_call x1, Pallas kernels, forward(): pl.pallas_call(functools.partial(fwd_kernel, n, n_tiles), grid=(n, n_tile...  90.5 us
    pallas_call x1, Pallas kernels, late(): pl.pallas_call(functools.partial(late_kernel, n), in_specs=[ANY, ANY, ANY...  30.3 us

profile of v3, /device:TPU:81, one launch (start us, length us, event | category | flops | bytes accessed | tf_op | source)
XLA Modules:
  0.0 249.8 jit_solution(3018085733586543583)
XLA Ops:
  0.6 1.7 copy.9.gain_hbm
  2.3 90.5 %head_fwd.1 = (f32[8,256,6144]{2,1,0:T(8,128)}, f32[8,256,6144]{2,1,0:T(8,128)}, bf16[8,960,512]{2,1,0:T(8,128)(2,1)}, s32[8,1,512]{2,1,0:T(1,128)}, f32[8,2,512]{2,1,0:T(2,128)}) custom-call(s32[1,512]{1,0:T(1,128)} %labels_hbm.1, bf16[960,512]{1,0:T(8,128)(2,1)} %bitcast.19, f32[960,1]{1,0:T(8,128)} %copy.9.gain_hbm, bf16[960,6144]{1,0:T(8,128)(2,1)} %bitcast.17), custom_call_target="tpu_custom_call" | custom-call | flops 48318382080 | bytes 100663296 | tf_op jit(solution)/shard_map/head_fwd/pallas_call | solution.py:221
  92.9 121.9 %head_bwd.1 = (f32[960,4096]{1,0:T(8,128)}, bf16[8,512,2048]{2,1,0:T(8,128)(2,1)}, bf16[960,512]{1,0:T(8,128)(2,1)}, f32[1,960]{1,0:T(1,128)}) custom-call(s32[8,1,512]{2,1,0:T(1,128)} %get-tuple-element.15.labels_hbm, f32[8,2,512]{2,1,0:T(2,128)} %get-tuple-element.14.stats_hbm, bf16[960,512]{1,0:T(8,128)(2,1)} %bitcast.20, f32[960,1]{1,0:T(8,128)} %copy.9.gain_hbm, ...), custom_call_target="tpu_custom_call" | custom-call | flops 96636764160 | bytes 100663296 | tf_op jit(solution)/shard_map/head_bwd/pallas_call | solution.py:404
  214.8 0.0 copy-start.1
  214.8 0.0 copy-start
  214.8 0.0 copy-start.2
  214.8 30.3 %head_dw.1 = f32[960,6144]{1,0:T(8,128)} custom-call(f32[960,4096]{1,0:T(8,128)} %get-tuple-element.20.early_hbm, bf16[8,960,512]{2,1,0:T(8,128)(2,1)} %get-tuple-element.16.normed_ref.normed_hbm, bf16[8,512,2048]{2,1,0:T(8,128)(2,1)} %get-tuple-element.21.dz_hbm), custom_call_target="tpu_custom_call" | custom-call | flops 16106127360 | bytes 47185920 | tf_op jit(solution)/shard_map/head_dw/pallas_call | solution.py:505
  245.2 0.0 copy-done.1
  245.2 0.6 fusion
  245.8 0.6 dynamic-slice_bitcast_fusion
  247.1 0.0 copy-done
  247.1 0.9 copy.13
  248.0 0.0 copy-done.2
  248.0 0.6 copy.14
Async XLA Ops:
  214.8 30.4 %copy-start.1 = (f32[8,2,512]{2,1,0:T(2,128)S(1)}, f32[8,2,512]{2,1,0:T(2,128)}, u32[]{:S(2)}) copy-start(f32[8,2,512]{2,1,0:T(2,128)} %get-tuple-element.14.stats_hbm) | copy-start | bytes 98308
  214.8 32.3 %copy-start = (bf16[960,512]{1,0:T(8,128)(2,1)S(1)}, bf16[960,512]{1,0:T(8,128)(2,1)}, u32[]{:S(2)}) copy-start(bf16[960,512]{1,0:T(8,128)(2,1)} %get-tuple-element.19) | copy-start | bytes 2949124
  214.8 33.2 %copy-start.2 = (f32[1,960]{1,0:T(1,128)S(1)}, f32[1,960]{1,0:T(1,128)}, u32[]{:S(2)}) copy-start(f32[1,960]{1,0:T(1,128)} %get-tuple-element.22) | copy-start | bytes 11524
